TPU v7x, 256 devices: a whole 4x4x8 slice. The times are simulated.
256 devices in a mesh: seq: 4 (over y), tp: 8 (over z), grp: 8 (over x, core).
Axes of the slice: x: 4, y: 4, z: 8, core: 2. Of those that a mesh axis runs over, the one named last changes fastest.
Arguments:
- queries: bfloat16 [16, 64, 128], P('grp', 'tp'), may hold values from -2000 to 2000
- cache_pool: bfloat16 [2048, 8, 2, 128, 128], P(('seq', 'grp'), 'tp'), may hold values from -6 to 6
- block_scale: bfloat16 [2048, 8, 2], P(('seq', 'grp'), 'tp'), may hold values from 0.29 to 3
- block_table: int32 [16, 128], replicated, may hold values from 0 to 2047, as said below
- lengths: int32 [16], replicated, may hold values from 128 to 16384
- output_weight: bfloat16 [8192, 8192], P('tp', ('seq', 'grp')), may hold values from -0.0625 to 0.0625
Outputs:
- attention_output: bfloat16 [16, 8192], P('tp', ('seq', 'grp'))
- decode_cache: bfloat16 [16, 128, 8, 2, 128, 128], P('grp', 'seq', 'tp')
- decode_scale: bfloat16 [16, 128, 8, 2], P('grp', 'seq', 'tp')
Inputs may be any that keep to these rules, and one draw needn't show every extreme that they name: block_table names every pool slot exactly once. Take any run of 64 slots starting at a multiple of 64, any group of 2 consecutive requests starting at a multiple of 2, and any range of 32 block positions starting at a multiple of 32: exactly 2 slots of the run hold blocks of those requests at those positions.
All inputs are finite; a program needn't handle non-finite values.
Results may differ from a plain program's by a relative error of at most 0.014.
Values may be sent and summed in bfloat16 or wider, within the bound.
A program may use at most 64 MiB of HBM per device.

v0:
```python
import math

import jax
import jax.numpy as jnp
from jax import lax
from jax.sharding import PartitionSpec as P

absent_score = -1e30


def sent_to_all(array, axis):
    length = lax.axis_size(axis)
    return lax.all_to_all(
        jnp.broadcast_to(array[None], (length, *array.shape)), axis, 0, 0, tiled=True
    )


def gathered_once(array, axis):
    leaves = jax.tree.leaves(array)
    sequence = sorted(range(len(leaves)), key=lambda k: -leaves[k].size)
    width = (1, *leaves[sequence[0]].shape)[-1]
    lines = [
        jnp.pad(leaves[k].reshape(-1), (0, -leaves[k].size % width)).reshape(-1, width)
        for k in sequence
    ]
    both, at, found = (sent_to_all(jnp.concatenate(lines), axis), 0, {})
    for k, line in zip(sequence, lines):
        share = both[:, at : at + len(line)].reshape(len(both), -1)
        found[k] = share[:, : leaves[k].size].reshape(-1, *leaves[k].shape)
        at += len(line)
    numbers = iter(range(len(leaves)))
    return jax.tree.map(lambda _: found[next(numbers)], array)


def joined_by_halves(pieces, combine):
    while len(jax.tree.leaves(pieces)[0]) > 1:
        pieces = jax.vmap(combine)(
            *(jax.tree.map(lambda part: part[side::2], pieces) for side in (0, 1))
        )
    return jax.tree.map(lambda part: part[0], pieces)


def joined_all(array, axis, combine):
    pieces = gathered_once(array, axis)
    return joined_by_halves(pieces, combine)


def in_order(pieces, dim):
    pieces = jnp.moveaxis(pieces, 0, dim)
    dims = pieces.shape
    return pieces.reshape(*dims[:dim], dims[dim] * dims[dim + 1], *dims[dim + 2 :])


def gather_directly(array, axis, dim):
    pieces = sent_to_all(array, axis)
    return in_order(pieces, dim)


def in_blocks(array, dim, length):
    dims = array.shape
    pieces = array.reshape(*dims[:dim], length, dims[dim] // length, *dims[dim + 1 :])
    return jnp.moveaxis(pieces, dim, 0)


def sum_at_owner(array, axis, dim):
    pieces = in_blocks(array, dim, lax.axis_size(axis))
    arrived = lax.all_to_all(pieces, axis, split_axis=0, concat_axis=0, tiled=True)
    return arrived.sum(axis=0)


def block_scores(block_queries, key_rows, key_scale, live_mask, root_scale):
    scores = jnp.einsum(
        "nkgd,nktd->nkgt", block_queries, key_rows, preferred_element_type=jnp.float32
    )
    scores = scores * key_scale[:, :, None, None] * root_scale
    return jnp.where(live_mask[:, None, None, :], scores, absent_score)


def block_terms(scores, peak_rows, live_mask, value_rows, value_scale):
    weight = jnp.where(live_mask[:, None, None, :], jnp.exp(scores - peak_rows[..., None]), 0.0)
    weight_sum = jnp.sum(weight, axis=-1)
    scaled = (weight * value_scale[:, :, None, None]).astype(jnp.bfloat16)
    partial_sum = jnp.einsum(
        "nkgt,nktd->nkgd", scaled, value_rows, preferred_element_type=jnp.float32
    )
    return (weight_sum, partial_sum)


def combine(former, latter):
    peak_former, sum_former, accum_former = former
    peak_latter, sum_latter, accum_latter = latter
    peak_both = jnp.maximum(peak_former, peak_latter)
    factor_former = jnp.exp(peak_former - peak_both)
    factor_latter = jnp.exp(peak_latter - peak_both)
    return (
        peak_both,
        sum_former * factor_former + sum_latter * factor_latter,
        accum_former * factor_former[..., None] + accum_latter * factor_latter[..., None],
    )


def per_device(queries, cache_pool, block_scale, block_table, lengths, output_weight):
    seq_count = lax.axis_size("seq")
    group_count = lax.axis_size("grp")
    seq_index = lax.axis_index("seq")
    group_index = lax.axis_index("grp")
    sources = seq_count * group_count
    pool_slots = cache_pool.shape[0]
    key_heads = cache_pool.shape[1]
    block_size = cache_pool.shape[3]
    head_size = cache_pool.shape[4]
    batch_rows, table_width = block_table.shape
    per_group = batch_rows // group_count
    share_blocks = table_width // seq_count
    capacity = pool_slots // sources
    heads_here = queries.shape[1]
    groups = heads_here // key_heads
    root_scale = 1.0 / math.sqrt(head_size)
    flat_ids = jnp.arange(batch_rows * table_width, dtype=jnp.int32)
    inverse = jnp.zeros_like(flat_ids).at[block_table.reshape(-1)].set(flat_ids)
    owner_ids = inverse.reshape(sources, pool_slots)
    owner_rows = owner_ids // table_width
    owner_cols = owner_ids % table_width
    destination = owner_cols // share_blocks * group_count + owner_rows // per_group
    slot_order = jnp.argsort(destination, axis=1, stable=True)
    source_index = seq_index * group_count + group_index
    local_order = lax.dynamic_index_in_dim(slot_order, source_index, 0, keepdims=False)
    outgoing_blocks = jnp.take(cache_pool, local_order, axis=0)
    outgoing_scales = jnp.take(block_scale, local_order, axis=0)
    sent_here = lax.dynamic_slice_in_dim(slot_order, source_index * capacity, capacity, 1)
    arrived_ids = jnp.take_along_axis(owner_ids, sent_here, axis=1).reshape(-1)
    arrived_rows = arrived_ids // table_width - group_index * per_group
    arrived_cols = arrived_ids % table_width - seq_index * share_blocks
    placement = jnp.argsort(arrived_rows * share_blocks + arrived_cols)
    arrived_blocks, arrived_scales = (
        lax.all_to_all(outgoing_blocks, ("seq", "grp"), split_axis=0, concat_axis=0, tiled=True),
        lax.all_to_all(outgoing_scales, ("seq", "grp"), split_axis=0, concat_axis=0, tiled=True),
    )
    decode_cache = jnp.take(arrived_blocks, placement, axis=0).reshape(
        (per_group, share_blocks) + arrived_blocks.shape[1:]
    )
    decode_scale = jnp.take(arrived_scales, placement, axis=0).reshape(
        (per_group, share_blocks) + arrived_scales.shape[1:]
    )
    own_lengths = lax.dynamic_slice_in_dim(lengths, group_index * per_group, per_group)
    block_queries = jnp.broadcast_to(
        queries.reshape(per_group, 1, key_heads, groups, head_size),
        (per_group, share_blocks, key_heads, groups, head_size),
    )
    block_queries = block_queries.reshape(pool_slots, key_heads, groups, head_size)
    block_starts = (
        seq_index * share_blocks + jnp.arange(share_blocks, dtype=jnp.int32)
    ) * block_size
    positions = block_starts[None, :, None] + jnp.arange(block_size, dtype=jnp.int32)[None, None, :]
    live_mask = (positions < own_lengths[:, None, None]).reshape(pool_slots, block_size)
    flat_cache = decode_cache.reshape((pool_slots,) + decode_cache.shape[2:])
    flat_scale = decode_scale.reshape((pool_slots,) + decode_scale.shape[2:]).astype(jnp.float32)
    scores = block_scores(
        block_queries, flat_cache[:, :, 0], flat_scale[:, :, 0], live_mask, root_scale
    )
    request_peak = jnp.max(
        scores.reshape(per_group, share_blocks, key_heads, groups, block_size), axis=(1, 4)
    )
    peak_rows = jnp.broadcast_to(
        request_peak[:, None], (per_group, share_blocks, key_heads, groups)
    )
    peak_rows = peak_rows.reshape(pool_slots, key_heads, groups)
    weight_sum, partial_sum = block_terms(
        scores, peak_rows, live_mask, flat_cache[:, :, 1], flat_scale[:, :, 1]
    )
    request_sum = jnp.sum(weight_sum.reshape(per_group, share_blocks, key_heads, groups), axis=1)
    request_accum = jnp.sum(
        partial_sum.reshape(per_group, share_blocks, key_heads, groups, head_size), axis=1
    )
    peak_all, sum_all, accum_all = joined_all(
        (request_peak, request_sum, request_accum), "seq", combine
    )
    attended = (
        (accum_all / sum_all[..., None])
        .astype(jnp.bfloat16)
        .reshape(per_group, heads_here * head_size)
    )
    partial_out = jnp.dot(
        gather_directly(attended, "grp", 0), output_weight, preferred_element_type=jnp.float32
    )
    summed = sum_at_owner(partial_out, "tp", 0)
    return (summed.astype(jnp.bfloat16), decode_cache, decode_scale)


def solution(mesh):
    placed = (
        P("grp", "tp", None),
        P(("seq", "grp"), "tp", None, None, None),
        P(("seq", "grp"), "tp", None),
        P(),
        P(),
        P("tp", ("seq", "grp")),
    )
    return jax.shard_map(
        per_device,
        mesh=mesh,
        in_specs=placed,
        out_specs=(
            P("tp", ("seq", "grp")),
            P("grp", "seq", "tp", None, None, None),
            P("grp", "seq", "tp", None),
        ),
        check_vma=False,
    )
```

profile of v0, /device:TPU:1, one launch (start us, length us, event | category | flops | bytes accessed | tf_op | source)
XLA Modules:
  0.0 140.6 jit_solution(6368246929354777386)
XLA Ops:
  0.7 0.8 compare_select_fusion
  1.4 8.0 %scatter_custom_fusion = s32[2048]{0:T(1024)S(1)} fusion(s32[2048]{0:T(1024)S(1)} %bitcast.102, s32[2048]{0:T(1024)S(1)} %iota.29, s32[]{:T(128)} %constant.120.clone.1), kind=kCustom, calls=%fused_computation.69 | custom fusion | bytes 8196 | tf_op jit(solution)/shard_map/scatter | solution.py:120
  9.7 1.0 sort.34
  10.7 0.2 dynamic-slice_reduce_fusion
  10.9 0.8 copy.97
  11.9 0.8 gather_fusion
  13.0 0.1 select_n.111
  13.1 0.6 gather_fusion.3
  13.9 0.7 copy.99
  14.6 8.6 %all-to-all-start.1 = ((bf16[64,1,2]{2,1,0:T(2,128)(2,1)}), bf16[64,1,2]{2,1,0:T(2,128)(2,1)S(1)}, u32[]{:S(2)}, u32[]{:S(2)}) async-start(bf16[64,1,2]{2,1,0:T(2,128)(2,1)} %copy.99), calls=%async_computation.1 | async-start | bytes 65536 | tf_op jit(solution)/shard_map/all_to_all | solution.py:137
  23.2 5.3 %gather_fusion.1 = bf16[64,2,128,128]{3,2,1,0:T(8,128)(2,1)} fusion(bf16[64,2,128,128]{3,2,1,0:T(8,128)(2,1)} %bitcast.96, s32[1024]{0:T(1024)S(1)} %pad_clamp_fusion.1), kind=kCustom, calls=%fused_computation.clone | custom fusion | bytes 8388864 | tf_op jit(solution)/shard_map/jit(_take)/gather | solution.py:128
  28.5 4.6 %bitcast_select_fusion.1 = bf16[64,1,2,128,128]{4,3,2,1,0:T(8,128)(2,1)} fusion(bf16[64,2,128,128]{3,2,1,0:T(8,128)(2,1)} %gather_fusion.1, pred[64]{0:T(512)(128)(4,1)S(1)} %compare_and_fusion.1), kind=kLoop, calls=%fused_computation.7 | loop fusion | flops 2097152 | bytes 8388672 | tf_op jit(solution)/shard_map/jit(_take)/select_n | solution.py:128
  33.1 7.6 %all-to-all-start = ((bf16[64,1,2,128,128]{4,3,2,1,0:T(8,128)(2,1)}), bf16[64,1,2,128,128]{4,3,2,1,0:T(8,128)(2,1)}, u32[]{:S(2)}, u32[]{:S(2)}) async-start(bf16[64,1,2,128,128]{4,3,2,1,0:T(8,128)(2,1)} %bitcast_select_fusion.1), calls=%async_computation | async-start | bytes 8388608 | tf_op jit(solution)/shard_map/all_to_all | solution.py:136
  41.0 2.0 %sort.35 = (s32[64]{0:T(128)}, s32[64]{0:T(128)S(1)}) sort(s32[64]{0:T(128)S(1)} %get-tuple-element.46, s32[64]{0:T(128)S(1)} %iota.31), dimensions={0}, to_apply=%region_2.4 | sort | flops 384 | bytes 1024 | tf_op jit(solution)/shard_map/jit(argsort)/sort | solution.py:134
  43.3 0.1 copy.101
  43.4 0.6 gather_fusion.4
  44.1 47.2 %all-to-all-done = bf16[64,1,2,128,128]{4,3,2,1,0:T(8,128)(2,1)} async-done(((bf16[64,1,2,128,128]{4,3,2,1,0:T(8,128)(2,1)}), bf16[64,1,2,128,128]{4,3,2,1,0:T(8,128)(2,1)}, u32[]{:S(2)}, u32[]{:S(2)}) %all-to-all-start) | async-done | bytes 4194336 | tf_op jit(solution)/shard_map/all_to_all | solution.py:136
  91.4 5.3 %gather_fusion.2 = bf16[64,2,128,128]{3,2,1,0:T(8,128)(2,1)} fusion(bf16[64,2,128,128]{3,2,1,0:T(8,128)(2,1)} %bitcast.6, s32[1024]{0:T(1024)S(1)} %pad_clamp_fusion), kind=kCustom, calls=%fused_computation.2.clone | custom fusion | bytes 8388864 | tf_op jit(solution)/shard_map/jit(_take)/gather | solution.py:139
  96.7 2.6 %bitcast_select_fusion = bf16[64,1,2,128,128]{4,3,0,2,1:T(8,128)(2,1)S(1)} fusion(bf16[64,2,128,128]{3,2,1,0:T(8,128)(2,1)} %gather_fusion.2, pred[64]{0:T(512)(128)(4,1)S(1)} %compare_and_fusion), kind=kLoop, calls=%fused_computation.6 | loop fusion | flops 2097152 | bytes 8388672 | tf_op jit(solution)/shard_map/jit(_take)/select_n | solution.py:139
  99.4 1.9 %copy-done.1 = bf16[64,1,2,128,128]{4,3,0,2,1:T(8,128)(2,1)} copy-done((bf16[64,1,2,128,128]{4,3,0,2,1:T(8,128)(2,1)}, bf16[64,1,2,128,128]{4,3,0,2,1:T(8,128)(2,1)S(1)}, u32[]{:S(2)}) %copy-start.1) | copy-done | bytes 4194328
  101.2 1.3 fusion.40
  102.6 0.2 fusion.8
  103.0 2.3 %bitcast_reduce_fusion = f32[2,8,128]{2,1,0:T(8,128)S(1)} fusion(bf16[64,1,2,128,128]{4,3,0,2,1:T(8,128)(2,1)} %copy-done.1, f32[64,8,128]{2,1,0:T(8,128)S(1)} %get-tuple-element.44, f32[64]{0:T(128)S(1)} %get-tuple-element.41, f32[64,8]{1,0:T(8,128)S(1)} %bitcast.99, pred[64,128]{1,0:T(8,128)(4,1)S(1)} %broadcast_compare_fusion), kind=kOutput, calls=%fused_computation.18 | convolution fusion | flops 17102848 | bytes 2377984 | tf_op jit(solution)/shard_map/nkgt,nktd->nkgd/dot_general | solution.py:83
  105.3 8.2 %all_to_all.25 = f32[4,18,128]{2,1,0:T(8,128)S(1)} all-to-all(f32[4,18,128]{2,1,0:T(8,128)S(1)} %broadcast_in_dim.85), channel_id=1, replica_groups=mesh['seq'=4,'tp'=8,'grp'=8] {'seq'}, dimensions={0} | all-to-all | bytes 73728 | tf_op jit(solution)/shard_map/all_to_all | solution.py:13
  114.0 10.4 %all_to_all.26 = bf16[8,2,1024]{2,1,0:T(2,128)(2,1)S(1)} all-to-all(bf16[8,2,1024]{2,1,0:T(2,128)(2,1)S(1)} %broadcast_in_dim.86), channel_id=1, replica_groups=mesh['seq'=4,'tp'=8,'grp'=8] {'grp'}, dimensions={0} | all-to-all | bytes 65536 | tf_op jit(solution)/shard_map/all_to_all | solution.py:13
  124.4 0.2 fusion.6
  124.6 0.6 copy.108
  125.2 8.2 %all-to-all-start.4 = ((f32[8,2,256]{2,1,0:T(2,128)}), f32[8,2,256]{2,1,0:T(2,128)S(1)}, u32[]{:S(2)}, u32[]{:S(2)}) async-start(f32[8,2,256]{2,1,0:T(2,128)} %copy.108), calls=%async_computation.4 | async-start | bytes 32768 | tf_op jit(solution)/shard_map/all_to_all | solution.py:67
  133.4 0.6 copy.110
  134.0 4.8 %copy.109 = bf16[2,32,1,2,128,128]{5,4,3,2,1,0:T(8,128)(2,1)} copy(bf16[2,32,1,2,128,128]{5,4,1,0,3,2:T(8,128)(2,1)} %bitcast.95) | data formatting | bytes 8388608
  138.8 1.2 all-to-all-done.4
  140.0 0.6 reduce_sum.39
  (62 shorter events, 2.3 us)
Async XLA Ops:
  0.6 123.8 %copy-start = (bf16[1024,256]{1,0:T(8,128)(2,1)S(1)}, bf16[1024,256]{1,0:T(8,128)(2,1)}, u32[]{:S(2)}) copy-start(bf16[1024,256]{1,0:T(8,128)(2,1)} %param.15) | copy-start | bytes 1572868
  14.6 18.5 %all-to-all-start.1 = ((bf16[64,1,2]{2,1,0:T(2,128)(2,1)}), bf16[64,1,2]{2,1,0:T(2,128)(2,1)S(1)}, u32[]{:S(2)}, u32[]{:S(2)}) async-start(bf16[64,1,2]{2,1,0:T(2,128)(2,1)} %copy.99), calls=%async_computation.1 | async-start | bytes 65536 | tf_op jit(solution)/shard_map/all_to_all | solution.py:137
  33.1 7.6 %copy-start.3 = (s32[16]{0:T(128)S(1)}, s32[16]{0:T(128)}, u32[]{:S(2)}) copy-start(s32[16]{0:T(128)} %param.14) | copy-start | bytes 196
  33.1 58.3 %all-to-all-start = ((bf16[64,1,2,128,128]{4,3,2,1,0:T(8,128)(2,1)}), bf16[64,1,2,128,128]{4,3,2,1,0:T(8,128)(2,1)}, u32[]{:S(2)}, u32[]{:S(2)}) async-start(bf16[64,1,2,128,128]{4,3,2,1,0:T(8,128)(2,1)} %bitcast_select_fusion.1), calls=%async_computation | async-start | bytes 8388608 | tf_op jit(solution)/shard_map/all_to_all | solution.py:136
  96.7 2.7 %copy-start.2 = (bf16[2,8,128]{2,1,0:T(8,128)(2,1)S(1)}, bf16[2,8,128]{2,1,0:T(8,128)(2,1)}, u32[]{:S(2)}) copy-start(bf16[2,8,128]{2,1,0:T(8,128)(2,1)} %param.10) | copy-start | bytes 12292
  99.3 1.9 %copy-start.1 = (bf16[64,1,2,128,128]{4,3,0,2,1:T(8,128)(2,1)}, bf16[64,1,2,128,128]{4,3,0,2,1:T(8,128)(2,1)S(1)}, u32[]{:S(2)}) copy-start(bf16[64,1,2,128,128]{4,3,0,2,1:T(8,128)(2,1)S(1)} %bitcast_select_fusion) | copy-start | bytes 12582916
  125.2 14.8 %all-to-all-start.4 = ((f32[8,2,256]{2,1,0:T(2,128)}), f32[8,2,256]{2,1,0:T(2,128)S(1)}, u32[]{:S(2)}, u32[]{:S(2)}) async-start(f32[8,2,256]{2,1,0:T(2,128)} %copy.108), calls=%async_computation.4 | async-start | bytes 32768 | tf_op jit(solution)/shard_map/all_to_all | solution.py:67
where the time goes:
time: 141 us
  waiting for transfers between devices  48.4 us (34%)
  local copies, waits for them, and re-layouts  32.1 us (23%)
  starting transfers between devices  24.3 us (17%)
  blocking collectives  18.6 us (13%)
  other arithmetic  12.5 us (9%)
  matrix products  3.74 us (3%)
    all_to_all x1, waiting for transfers between devices, per_device(): lax.all_to_all(outgoing_blocks, ('seq', 'grp'), split_axis=0, concat_axis...  47.2 us
    all_to_all x2, blocking collectives, sent_to_all(): lax.all_to_all(jnp.broadcast_to(array[None], (length, *array.shape)), axi...  18.6 us
    all_to_all x1, starting transfers between devices, per_device(): lax.all_to_all(outgoing_scales, ('seq', 'grp'), split_axis=0, concat_axis...  8.58 us
    all_to_all x1, starting transfers between devices, sum_at_owner(): lax.all_to_all(pieces, axis, split_axis=0, concat_axis=0, tiled=True)  8.19 us
    scatter x1, local copies, waits for them, and re-layouts, per_device(): inverse = jnp.zeros_like(flat_ids).at[block_table.reshape(-1)].set(flat_ids)  8.05 us
    all_to_all x1, starting transfers between devices, per_device(): lax.all_to_all(outgoing_blocks, ('seq', 'grp'), split_axis=0, concat_axis...  7.57 us
    unnamed x11, local copies, waits for them, and re-layouts  7.33 us
    gather x1, local copies, waits for them, and re-layouts, per_device(): outgoing_blocks = jnp.take(cache_pool, local_order, axis=0)  5.29 us
  transfers between devices with their start and end apart: 3, of which 2 were waited for; matrix products, arithmetic and copies ran while one was open for 13% of the time, Pallas kernels for 0%

commit v1 on v0

v1 whole, which is shorter than its diff:
```python
import functools
import math

import jax
import jax.numpy as jnp
from jax import lax
from jax.experimental import pallas as pl
from jax.experimental.pallas import tpu as pltpu
from jax.sharding import PartitionSpec as P

MESH = pl.DeviceIdType.MESH
ABSENT = -1e30
NSEQ, NTP, NGRP = 4, 8, 8
NDEV = NSEQ * NGRP
BLK = 128
ROOT = 1.0 / math.sqrt(128.0)
START = (0, 256, 128, 384)


def spread(i):
    turn, rest = i // 8, i % 8
    dy, dc = rest // 2, rest % 2
    return dy, (dy + turn) % 4, dc


def exchange_kernel(
    idx, scal, pool_hbm, q_ref, w_hbm, place_ref,
    arr, out_ref, scale_out,
    pool_k, pool_v, send, qall, w, pmsg, part, amsg, att, pout, zbuf,
    pool_sem, w_sem, q_ssem, q_rsem, b_ssem, b_rsem, p_ssem, p_rsem, a_ssem, a_rsem, z_ssem, z_rsem,
):
    y = lax.axis_index("seq")
    z = lax.axis_index("tp")
    g = lax.axis_index("grp")
    me = y * NGRP + g

    def peer(i):
        dy, dx, dc = spread(i)
        ty = (y + dy) % 4
        tg = ((g // 2 + dx) % 4) * 2 + (g + dc) % 2
        return ty, tg

    barrier = pltpu.get_barrier_semaphore()

    def greet(i, carry):
        ty, tg = peer(i)
        pl.semaphore_signal(barrier, inc=1, device_id={"seq": ty, "grp": tg}, device_id_type=MESH)
        return carry

    lax.fori_loop(1, NDEV, greet, 0)

    def greet_z(i, carry):
        pl.semaphore_signal(barrier, inc=1, device_id={"tp": (z + i) % NTP}, device_id_type=MESH)
        return carry

    lax.fori_loop(1, NTP, greet_z, 0)

    keys_in = pltpu.make_async_copy(pool_hbm.at[:, pl.ds(0, BLK)], pool_k, pool_sem.at[0])
    vals_in = pltpu.make_async_copy(pool_hbm.at[:, pl.ds(BLK, BLK)], pool_v, pool_sem.at[1])
    w_in = pltpu.make_async_copy(w_hbm, w, w_sem)
    keys_in.start()
    vals_in.start()
    w_in.start()
    qall[g] = q_ref[...]

    def pick(c):
        pool, r = (pool_k, pool_v)[c // 2], c % 2

        def body(t, carry):
            slot = idx[2 * t + r]
            send[t, pl.ds(START[c], BLK), :] = pool[slot]
            return carry

        lax.fori_loop(0, NDEV, body, 0)

    def block_copy(c, i):
        ty, tg = peer(i)
        rows = pl.ds(START[c], BLK)
        return pltpu.make_async_remote_copy(
            src_ref=send.at[ty * NGRP + tg, rows],
            dst_ref=arr.at[me, rows],
            send_sem=b_ssem.at[c, i],
            recv_sem=b_rsem.at[c, i],
            device_id={"seq": ty, "grp": tg},
            device_id_type=MESH,
        )

    def send_wave(c):
        def body(i, carry):
            block_copy(c, i).start()
            return carry

        lax.fori_loop(1, NDEV, body, 0)

    def q_copy(i):
        tg = (g + i) % NGRP
        return pltpu.make_async_remote_copy(
            src_ref=q_ref, dst_ref=qall.at[g], send_sem=q_ssem.at[i], recv_sem=q_rsem.at[i],
            device_id={"grp": tg}, device_id_type=MESH,
        )

    keys_in.wait()
    pick(0)
    pl.semaphore_wait(barrier, NDEV - 1 + NTP - 1)
    for i in range(1, NGRP):
        q_copy(i).start()
    send_wave(0)
    pick(1)
    vals_in.wait()
    pick(2)
    pick(3)
    for i in range(1, NGRP):
        q_copy(i).wait()

    row16 = lax.broadcasted_iota(jnp.int32, (16, BLK), 0)
    lane16 = lax.broadcasted_iota(jnp.int32, (16, BLK), 1)
    row4 = lax.broadcasted_iota(jnp.int32, (4, BLK), 0)
    lane4 = lax.broadcasted_iota(jnp.int32, (4, BLK), 1)

    def attend(gg, carry):
        q = qall[gg]
        scores, masks = [], []
        for n in range(8):
            t, r = (n // 2) * NGRP + gg, n % 2
            k = 2 * t + r
            keys = send[t, pl.ds(r * 256, BLK), :]
            s = lax.dot_general(q, keys, (((1,), (1,)), ((), ())), preferred_element_type=jnp.float32)
            s = s * (scal[k] * ROOT)
            limit = jnp.where(row16 < 8, idx[64 + k], idx[128 + k])
            live = lane16 < limit
            scores.append(jnp.where(live, s, ABSENT))
            masks.append(live)
        top = functools.reduce(jnp.maximum, scores)
        peak = jnp.max(top, axis=1, keepdims=True)
        total = jnp.zeros((16, BLK), jnp.float32)
        acc = jnp.zeros((16, BLK), jnp.float32)
        for n in range(8):
            t, r = (n // 2) * NGRP + gg, n % 2
            k = 2 * t + r
            weight = jnp.where(masks[n], jnp.exp(scores[n] - peak), 0.0)
            total = total + weight
            scaled = (weight * scal[64 + k]).astype(jnp.bfloat16)
            acc = acc + jnp.dot(scaled, send[t, pl.ds(r * 256 + BLK, BLK), :], preferred_element_type=jnp.float32)
        denom = jnp.sum(total, axis=1, keepdims=True)
        stats = jnp.where(lane16 == 2, peak, jnp.where(lane16 == 3, denom, 0.0))
        for qq in range(NSEQ):
            t = qq * NGRP + gg
            pmsg[t, pl.ds(0, 4), :] = acc[4 * qq : 4 * qq + 4]
            low = stats[4 * qq : 4 * qq + 4]
            for r in range(2):
                k = 2 * t + r
                low = jnp.where((row4 == r) & (lane4 == 0), scal[k], low)
                low = jnp.where((row4 == r) & (lane4 == 1), scal[64 + k], low)
            pmsg[t, pl.ds(4, 4), :] = low
        return carry

    lax.fori_loop(0, NGRP, attend, 0)

    def p_copy(i):
        ty, tg = peer(i)
        return pltpu.make_async_remote_copy(
            src_ref=pmsg.at[ty * NGRP + tg], dst_ref=part.at[me],
            send_sem=p_ssem.at[i], recv_sem=p_rsem.at[i],
            device_id={"seq": ty, "grp": tg}, device_id_type=MESH,
        )

    def a_copy(i):
        ty, tg = peer(i)
        return pltpu.make_async_remote_copy(
            src_ref=amsg, dst_ref=att.at[(y % 2) * 16 + g * 2 + y // 2],
            send_sem=a_ssem.at[i], recv_sem=a_rsem.at[i],
            device_id={"seq": ty, "grp": tg}, device_id_type=MESH,
        )

    def each(make, what, first, last):
        def body(i, carry):
            getattr(make(i), what)()
            return carry

        lax.fori_loop(first, last, body, 0)

    each(p_copy, "start", 1, NDEV)
    part[me] = pmsg[me]
    send_wave(1)
    each(p_copy, "wait", 1, NDEV)

    peaks = part[:, pl.ds(4, 4), 2:3]
    sums = part[:, pl.ds(4, 4), 3:4]
    peak = jnp.max(peaks, axis=0, keepdims=True)
    factor = jnp.exp(peaks - peak)
    denom = jnp.sum(sums * factor, axis=0)
    numer = jnp.sum(part[:, pl.ds(0, 4), :] * factor, axis=0)
    rows = (numer / denom).astype(jnp.bfloat16).astype(jnp.float32)
    amsg[...] = rows
    att[(y % 2) * 16 + g * 2 + y // 2] = rows
    lanes = lax.broadcasted_iota(jnp.int32, (64, 256), 1)
    at = place_ref[...]
    hot = (lanes == (at // 2) * 8 + 4 + at % 2).astype(jnp.float32).astype(jnp.bfloat16)
    picked = jnp.dot(hot, part[...].reshape(256, BLK).astype(jnp.bfloat16), preferred_element_type=jnp.float32)
    scale_out[...] = picked[:, 0:2].astype(jnp.bfloat16)

    each(a_copy, "start", 1, NDEV)
    send_wave(2)
    send_wave(3)
    arr[me] = send[me]
    w_in.wait()
    each(a_copy, "wait", 1, NDEV)

    total = jnp.zeros((16, 256), jnp.float32)
    for h in range(8):
        lhs = att[pl.ds((h // 4) * 16, 16), h % 4, :].astype(jnp.bfloat16)
        total = total + jnp.dot(lhs, w[pl.ds(h * BLK, BLK), :], preferred_element_type=jnp.float32)
    for k in range(NTP):
        pout[k] = total[2 * k : 2 * k + 2]

    def z_copy(i):
        tz = (z + i) % NTP
        return pltpu.make_async_remote_copy(
            src_ref=pout.at[tz], dst_ref=zbuf.at[z], send_sem=z_ssem.at[i], recv_sem=z_rsem.at[i],
            device_id={"tp": tz}, device_id_type=MESH,
        )

    each(z_copy, "start", 1, NTP)
    zbuf[z] = pout[z]
    each(z_copy, "wait", 1, NTP)
    out_ref[...] = jnp.sum(zbuf[...], axis=0).astype(jnp.bfloat16)

    for c in range(4):
        each(functools.partial(block_copy, c), "wait", 1, NDEV)


def place_kernel(src, arr, out, sem):
    for p in range(64):
        pltpu.make_async_copy(arr.at[src[p]], out.at[p], sem).start()
    pltpu.make_async_copy(arr, out, sem).wait()


def per_device(queries, cache_pool, block_scale, block_table, lengths, output_weight):
    y = lax.axis_index("seq")
    g = lax.axis_index("grp")
    me = y * NGRP + g
    table = block_table.reshape(NGRP, 2, NSEQ, 32).transpose(2, 0, 1, 3).reshape(NDEV, 64)
    spot = jnp.arange(64, dtype=jnp.int32)[None]
    code = (table % 64) * 64 + spot
    mine = table // 64 == me
    low = jnp.min(jnp.where(mine, code, 1 << 20), axis=1)
    high = jnp.max(jnp.where(mine, code, -1), axis=1)
    codes = jnp.stack([low, high], axis=1)
    slots = codes // 64
    second = codes % 64 // 32
    column = (jnp.arange(NDEV, dtype=jnp.int32) // NGRP)[:, None] * 32 + codes % 32
    pairs = jnp.tile(lengths.reshape(NGRP, 2), (NSEQ, 1))
    length = jnp.where(second == 0, pairs[:, :1], pairs[:, 1:])
    limit = jnp.clip(length - column * BLK, 0, BLK)
    idx = jnp.concatenate([
        slots.reshape(-1),
        jnp.where(second == 0, limit, 0).reshape(-1),
        jnp.where(second == 1, limit, 0).reshape(-1),
    ])
    chosen = slots.reshape(-1)[:, None] == jnp.arange(64, dtype=jnp.int32)[None]
    scales = block_scale.reshape(64, 2).astype(jnp.float32)
    scal = jnp.sum(jnp.where(chosen[None], scales.T[:, None, :], 0.0), axis=2).reshape(-1)
    own = lax.dynamic_slice(block_table, (2 * g, 32 * y), (2, 32)).reshape(64)
    before = (own[None, :] // 64 == own[:, None] // 64) & (own[None, :] < own[:, None])
    place = (own // 64) * 2 + jnp.sum(before.astype(jnp.int32), axis=1)

    vmem = pl.BlockSpec(memory_space=pltpu.VMEM)
    smem = pl.BlockSpec(memory_space=pltpu.SMEM)
    hbm = pl.BlockSpec(memory_space=pl.ANY)
    dma = pltpu.SemaphoreType.DMA
    arrived, summed, decode_scale = pl.pallas_call(
        exchange_kernel,
        out_shape=(
            jax.ShapeDtypeStruct((NDEV, 512, BLK), jnp.bfloat16),
            jax.ShapeDtypeStruct((2, 256), jnp.bfloat16),
            jax.ShapeDtypeStruct((64, 2), jnp.bfloat16),
        ),
        in_specs=[smem, smem, hbm, vmem, hbm, vmem],
        out_specs=(vmem, vmem, vmem),
        scratch_shapes=[
            pltpu.VMEM((64, BLK, BLK), jnp.bfloat16),
            pltpu.VMEM((64, BLK, BLK), jnp.bfloat16),
            pltpu.VMEM((NDEV, 512, BLK), jnp.bfloat16),
            pltpu.VMEM((NGRP, 16, BLK), jnp.bfloat16),
            pltpu.VMEM((1024, 256), jnp.bfloat16),
            pltpu.VMEM((NDEV, 8, BLK), jnp.float32),
            pltpu.VMEM((NDEV, 8, BLK), jnp.float32),
            pltpu.VMEM((4, BLK), jnp.float32),
            pltpu.VMEM((NDEV, 4, BLK), jnp.float32),
            pltpu.VMEM((NTP, 2, 256), jnp.float32),
            pltpu.VMEM((NTP, 2, 256), jnp.float32),
            dma((2,)), dma, dma((NGRP,)), dma((NGRP,)),
            dma((4, NDEV)), dma((4, NDEV)),
            dma((NDEV,)), dma((NDEV,)), dma((NDEV,)), dma((NDEV,)),
            dma((NTP,)), dma((NTP,)),
        ],
        compiler_params=pltpu.CompilerParams(collective_id=0, has_side_effects=True),
    )(
        idx, scal, cache_pool.reshape(64, 256, BLK), queries.reshape(16, BLK), output_weight, place[:, None],
    )
    decode_cache = pl.pallas_call(
        place_kernel,
        out_shape=jax.ShapeDtypeStruct((64, 256, BLK), jnp.bfloat16),
        in_specs=[smem, vmem],
        out_specs=hbm,
        scratch_shapes=[dma],
    )(place, arrived.reshape(64, 256, BLK))
    return (
        summed,
        decode_cache.reshape(2, 32, 1, 2, BLK, BLK),
        decode_scale.reshape(2, 32, 1, 2),
    )


def solution(mesh):
    placed = (
        P("grp", "tp", None),
        P(("seq", "grp"), "tp", None, None, None),
        P(("seq", "grp"), "tp", None),
        P(),
        P(),
        P("tp", ("seq", "grp")),
    )
    return jax.shard_map(
        per_device,
        mesh=mesh,
        in_specs=placed,
        out_specs=(
            P("tp", ("seq", "grp")),
            P("grp", "seq", "tp", None, None, None),
            P("grp", "seq", "tp", None),
        ),
        check_vma=False,
    )
```

time: 141 us -> 82.2 us (0.58)
  Pallas kernels: 0 us -> 72.2 us
  waiting for transfers between devices: 48.4 us -> 0 us
  local copies, waits for them, and re-layouts: 32.1 us -> 5.64 us
  starting transfers between devices: 24.3 us -> 0 us
  blocking collectives: 18.6 us -> 0 us
  other arithmetic: 12.5 us -> 3.32 us
  matrix products: 3.74 us -> 0 us
    pallas_call x0 -> x2, Pallas kernels: none -> 72.2 us  [the longest x1 68 us: per_device(): pl.pallas_call(exchange_kernel, out_shape=(jax.ShapeDtypeStruct((NDEV, 51...]
    all_to_all x3 -> x0, waiting for transfers between devices: 48.4 us -> none  [the longest x1 47.2 us: per_device(): lax.all_to_all(outgoing_blocks, ('seq', 'grp'), split_axis=0, concat_axis...]
    all_to_all x3 -> x0, starting transfers between devices: 24.3 us -> none  [the longest x1 8.58 us: per_device(): lax.all_to_all(outgoing_scales, ('seq', 'grp'), split_axis=0, concat_axis...]
    all_to_all x2 -> x0, blocking collectives: 18.6 us -> none  [sent_to_all(): lax.all_to_all(jnp.broadcast_to(array[None], (length, *array.shape)), axi...]
    gather x11 -> x0, local copies, waits for them, and re-layouts: 13.2 us -> none  [the longest x1 5.29 us: per_device(): outgoing_blocks = jnp.take(cache_pool, local_order, axis=0)]
    scatter x1 -> x0, local copies, waits for them, and re-layouts: 8.05 us -> none  [per_device(): inverse = jnp.zeros_like(flat_ids).at[block_table.reshape(-1)].set(flat_ids)]
    select_n x7 -> x3, other arithmetic: 8.08 us -> 0.04 us  [the longest x1 0.02 us: per_device(): jnp.where(second == 0, limit, 0).reshape(-1)]
    unnamed x11 -> x6, local copies, waits for them, and re-layouts: 7.33 us -> 1.23 us
  transfers between devices with their start and end apart: 3 -> 0, of which waited for: 2 -> 0; matrix products, arithmetic and copies ran while one was open for 13% -> 0% of each run, Pallas kernels for 0% -> 0%
where the time goes in v1:
time: 82.2 us; the launch traced here: 81.9 us
  Pallas kernels  72.2 us (88%)
  local copies, waits for them, and re-layouts  5.64 us (7%)
  other arithmetic  3.32 us (4%)
    pallas_call x1, Pallas kernels, per_device(): pl.pallas_call(exchange_kernel, out_shape=(jax.ShapeDtypeStruct((NDEV, 51...  68 us
    pallas_call x1, Pallas kernels, per_device(): pl.pallas_call(place_kernel, out_shape=jax.ShapeDtypeStruct((64, 256, BLK...  4.17 us

profile of v1, /device:TPU:1, one launch (start us, length us, event | category | flops | bytes accessed | tf_op | source)
XLA Modules:
  0.0 81.9 jit_solution(9989776412290356658)
XLA Ops:
  0.6 0.8 dynamic_slice.3
  1.4 0.1 broadcast_in_dim_reshape.2
  1.5 0.2 convert_reduce_fusion
  1.7 0.6 multiply_add_fusion.1.src
  2.3 0.7 convert_bitcast_fusion
  3.0 0.7 tile.10
  3.7 0.1 copy.56
  3.8 0.1 tile.12
  3.9 0.1 broadcast_in_dim.63
  3.9 0.1 broadcast_in_dim.64
  4.1 0.1 add.113
  4.1 0.1 add.114
  4.3 0.1 broadcast_in_dim.61
  4.4 0.1 reshape.319
  4.5 0.1 copy.62
  4.6 0.6 fusion.5.place_ref
  5.3 0.8 reshape.310
  6.0 0.4 select_reduce_fusion.2
  6.4 0.1 copy.53
  6.5 0.1 stack.11
  6.6 0.1 copy.54
  6.7 0.1 stack.12
  6.8 0.1 copy.55
  6.9 0.1 stack.14
  7.0 0.6 pad_add_fusion.1.idx
  7.7 0.1 iota_compare_fusion
  7.7 0.1 select_reduce_fusion
  7.8 0.6 reshape.311.scal
  8.4 68.0 %shard_map.85 = (bf16[32,512,128]{2,1,0:T(8,128)(2,1)}, bf16[2,256]{1,0:T(2,128)(2,1)}, bf16[64,2]{1,0:T(8,128)(2,1)}) custom-call(s32[192]{0:T(256)} %pad_add_fusion.1.idx, f32[128]{0:T(128)} %reshape.311.scal, bf16[64,256,128]{2,1,0:T(8,128)(2,1)} %bitcast.43, bf16[16,128]{1,0:T(8,128)(2,1)} %bitcast.47, bf16[1024,256]{1,0:T(8,128)(2,1)} %w_hbm.1, ...), custom_call_target="tpu_custom_call" | custom-call | tf_op jit(solution)/shard_map/pallas_call | solution.py:271
  76.5 4.2 %shard_map.86 = bf16[64,256,128]{2,1,0:T(8,128)(2,1)} custom-call(s32[64]{0:T(128)} %multiply_add_fusion.1.src, bf16[64,256,128]{2,1,0:T(8,128)(2,1)} %bitcast.45), custom_call_target="tpu_custom_call" | custom-call | tf_op jit(solution)/shard_map/pallas_call | solution.py:301
  80.7 0.7 copy.65
  81.3 0.6 copy.70
  (13 shorter events, 0.2 us)
Async XLA Ops:
  76.5 4.2 %copy-start = (bf16[64,2]{1,0:T(8,128)(2,1)S(1)}, bf16[64,2]{1,0:T(8,128)(2,1)}, u32[]{:S(2)}) copy-start(bf16[64,2]{1,0:T(8,128)(2,1)} %get-tuple-element.8) | copy-start | bytes 772
  76.5 4.9 %copy-start.1 = (bf16[2,256]{1,0:T(2,128)(2,1)S(1)}, bf16[2,256]{1,0:T(2,128)(2,1)}, u32[]{:S(2)}) copy-start(bf16[2,256]{1,0:T(2,128)(2,1)} %get-tuple-element.35) | copy-start | bytes 3076

commit v2 on v1

--- a/solution.py
+++ b/solution.py
@@ -24,10 +24,11 @@
 
 
 def exchange_kernel(
-    idx, scal, pool_hbm, q_ref, w_hbm, place_ref,
-    arr, out_ref, scale_out,
-    pool_k, pool_v, send, qall, w, pmsg, part, amsg, att, pout, zbuf,
-    pool_sem, w_sem, q_ssem, q_rsem, b_ssem, b_rsem, p_ssem, p_rsem, a_ssem, a_rsem, z_ssem, z_rsem,
+    table_hbm, lengths_hbm, scale_hbm, pool_hbm, q_hbm, w_hbm,
+    arr, out_ref, scale_out, place_out,
+    table, scale_in, codes_v, scales_v, codes, scal, lens,
+    pool_k, pool_v, send, q_ref, qall, w, pmsg, part, amsg, att, pout, zbuf,
+    in_sem, q_ssem, q_rsem, b_ssem, b_rsem, p_ssem, p_rsem, a_ssem, a_rsem, z_ssem, z_rsem,
 ):
     y = lax.axis_index("seq")
     z = lax.axis_index("tp")
@@ -40,6 +41,18 @@
         tg = ((g // 2 + dx) % 4) * 2 + (g + dc) % 2
         return ty, tg
 
+    table_in = pltpu.make_async_copy(table_hbm, table, in_sem.at[0])
+    keys_in = pltpu.make_async_copy(pool_hbm.at[:, pl.ds(0, BLK)], pool_k, in_sem.at[1])
+    vals_in = pltpu.make_async_copy(pool_hbm.at[:, pl.ds(BLK, BLK)], pool_v, in_sem.at[2])
+    q_in = pltpu.make_async_copy(q_hbm, q_ref, in_sem.at[3])
+    scales_in = pltpu.make_async_copy(scale_hbm, scale_in, in_sem.at[4])
+    lens_in = pltpu.make_async_copy(lengths_hbm, lens, in_sem.at[5])
+    w_in = pltpu.make_async_copy(w_hbm, w, in_sem.at[6])
+    codes_out = pltpu.make_async_copy(codes_v, codes, in_sem.at[7])
+    scales_out = pltpu.make_async_copy(scales_v, scal, in_sem.at[8])
+    for copy in (table_in, q_in, keys_in, scales_in, lens_in, vals_in, w_in):
+        copy.start()
+
     barrier = pltpu.get_barrier_semaphore()
 
     def greet(i, carry):
@@ -55,19 +68,38 @@
 
     lax.fori_loop(1, NTP, greet_z, 0)
 
-    keys_in = pltpu.make_async_copy(pool_hbm.at[:, pl.ds(0, BLK)], pool_k, pool_sem.at[0])
-    vals_in = pltpu.make_async_copy(pool_hbm.at[:, pl.ds(BLK, BLK)], pool_v, pool_sem.at[1])
-    w_in = pltpu.make_async_copy(w_hbm, w, w_sem)
-    keys_in.start()
-    vals_in.start()
-    w_in.start()
+    row16 = lax.broadcasted_iota(jnp.int32, (16, BLK), 0)
+    lane16 = lax.broadcasted_iota(jnp.int32, (16, BLK), 1)
+    table_in.wait()
+    names = table[...]
+    code = (names & 63) * 64 + (row16 & 1) * 32 + (lane16 & 31)
+    mine = (names >> 6) == me
+    low = jnp.where(mine, code, 8191)
+    high = jnp.where(mine, code, -1)
+    found = jnp.zeros((16, BLK), jnp.int32)
+    for qq in range(NSEQ):
+        part_of = (lane16 >> 5) == qq
+        least = jnp.min(jnp.where(part_of, low, 8191), axis=1, keepdims=True)
+        most = jnp.max(jnp.where(part_of, high, -1), axis=1, keepdims=True)
+        found = jnp.where(lane16 == qq, least, jnp.where(lane16 == 4 + qq, most, found))
+    other = pltpu.roll(found, 15, 0)
+    codes_v[...] = jnp.where(lane16 < 4, jnp.minimum(found, other), jnp.maximum(found, other))
+    codes_out.start()
+    q_in.wait()
     qall[g] = q_ref[...]
+    scales_in.wait()
+    scales_v[...] = scale_in[...].astype(jnp.float32)
+    scales_out.start()
+    codes_out.wait()
+
+    def code_of(q, gg, r):
+        return codes[2 * gg, q + 4 * r]
 
     def pick(c):
         pool, r = (pool_k, pool_v)[c // 2], c % 2
 
         def body(t, carry):
-            slot = idx[2 * t + r]
+            slot = (code_of(t // NGRP, t % NGRP, r) >> 6) & 63
             send[t, pl.ds(START[c], BLK), :] = pool[slot]
             return carry
 
@@ -109,24 +141,27 @@
     vals_in.wait()
     pick(2)
     pick(3)
+    scales_out.wait()
+    lens_in.wait()
     for i in range(1, NGRP):
         q_copy(i).wait()
 
-    row16 = lax.broadcasted_iota(jnp.int32, (16, BLK), 0)
-    lane16 = lax.broadcasted_iota(jnp.int32, (16, BLK), 1)
     row4 = lax.broadcasted_iota(jnp.int32, (4, BLK), 0)
     lane4 = lax.broadcasted_iota(jnp.int32, (4, BLK), 1)
 
     def attend(gg, carry):
         q = qall[gg]
-        scores, masks = [], []
+        scores, masks, key_scales, value_scales = [], [], [], []
         for n in range(8):
             t, r = (n // 2) * NGRP + gg, n % 2
-            k = 2 * t + r
+            found_at = code_of(n // 2, gg, r)
+            slot, row, column = (found_at >> 6) & 63, (found_at >> 5) & 1, (n // 2) * 32 + (found_at & 31)
             keys = send[t, pl.ds(r * 256, BLK), :]
             s = lax.dot_general(q, keys, (((1,), (1,)), ((), ())), preferred_element_type=jnp.float32)
-            s = s * (scal[k] * ROOT)
-            limit = jnp.where(row16 < 8, idx[64 + k], idx[128 + k])
+            s = s * (scal[0, slot] * ROOT)
+            value_scales.append(scal[1, slot])
+            key_scales.append(scal[0, slot])
+            limit = jnp.where((row16 >> 3) == row, lens[2 * gg + row] - column * BLK, 0)
             live = lane16 < limit
             scores.append(jnp.where(live, s, ABSENT))
             masks.append(live)
@@ -136,10 +171,9 @@
         acc = jnp.zeros((16, BLK), jnp.float32)
         for n in range(8):
             t, r = (n // 2) * NGRP + gg, n % 2
-            k = 2 * t + r
             weight = jnp.where(masks[n], jnp.exp(scores[n] - peak), 0.0)
             total = total + weight
-            scaled = (weight * scal[64 + k]).astype(jnp.bfloat16)
+            scaled = (weight * value_scales[n]).astype(jnp.bfloat16)
             acc = acc + jnp.dot(scaled, send[t, pl.ds(r * 256 + BLK, BLK), :], preferred_element_type=jnp.float32)
         denom = jnp.sum(total, axis=1, keepdims=True)
         stats = jnp.where(lane16 == 2, peak, jnp.where(lane16 == 3, denom, 0.0))
@@ -148,9 +182,8 @@
             pmsg[t, pl.ds(0, 4), :] = acc[4 * qq : 4 * qq + 4]
             low = stats[4 * qq : 4 * qq + 4]
             for r in range(2):
-                k = 2 * t + r
-                low = jnp.where((row4 == r) & (lane4 == 0), scal[k], low)
-                low = jnp.where((row4 == r) & (lane4 == 1), scal[64 + k], low)
+                low = jnp.where((row4 == r) & (lane4 == 0), key_scales[2 * qq + r], low)
+                low = jnp.where((row4 == r) & (lane4 == 1), value_scales[2 * qq + r], low)
             pmsg[t, pl.ds(4, 4), :] = low
         return carry
 
@@ -193,16 +226,26 @@
     rows = (numer / denom).astype(jnp.bfloat16).astype(jnp.float32)
     amsg[...] = rows
     att[(y % 2) * 16 + g * 2 + y // 2] = rows
-    lanes = lax.broadcasted_iota(jnp.int32, (64, 256), 1)
-    at = place_ref[...]
-    hot = (lanes == (at // 2) * 8 + 4 + at % 2).astype(jnp.float32).astype(jnp.bfloat16)
-    picked = jnp.dot(hot, part[...].reshape(256, BLK).astype(jnp.bfloat16), preferred_element_type=jnp.float32)
-    scale_out[...] = picked[:, 0:2].astype(jnp.bfloat16)
-
     each(a_copy, "start", 1, NDEV)
     send_wave(2)
     send_wave(3)
     arr[me] = send[me]
+    wide = lax.broadcasted_iota(jnp.int32, (8, BLK), 1)
+    first = pltpu.roll(jnp.broadcast_to(table[pl.ds(2 * g, 1), :], (8, BLK)), (BLK - 32 * y) % BLK, 1)
+    second = pltpu.roll(jnp.broadcast_to(table[pl.ds(2 * g + 1, 1), :], (8, BLK)), (BLK + 32 - 32 * y) % BLK, 1)
+    own = jnp.where(wide < 32, first, second)[0:1]
+    across = jnp.broadcast_to(own, (BLK, BLK))
+    down = across.T
+    inside = lax.broadcasted_iota(jnp.int32, (BLK, BLK), 0) < 64
+    before = inside & ((down >> 6) == (across >> 6)) & (down < across)
+    rank = jnp.sum(before.astype(jnp.int32), axis=0, keepdims=True)
+    place_out[...] = ((own >> 6) * 2 + rank) & 63
+    lines = lax.broadcasted_iota(jnp.int32, (256, BLK), 0)
+    hot = (lines == (own >> 6) * 8 + 4 + rank).astype(jnp.float32).astype(jnp.bfloat16)
+    flat = part[...].reshape(256, BLK).T[0:8].astype(jnp.bfloat16)
+    picked = jnp.dot(flat, hot, preferred_element_type=jnp.float32).astype(jnp.bfloat16)
+    scale_out[0] = picked[0:2, 0:32]
+    scale_out[1] = picked[0:2, 32:64]
     w_in.wait()
     each(a_copy, "wait", 1, NDEV)
 
@@ -229,58 +272,52 @@
         each(functools.partial(block_copy, c), "wait", 1, NDEV)
 
 
-def place_kernel(src, arr, out, sem):
-    for p in range(64):
-        pltpu.make_async_copy(arr.at[src[p]], out.at[p], sem).start()
-    pltpu.make_async_copy(arr, out, sem).wait()
+def place_kernel(src, arr, summed, scales, out, out_sum, out_scales, sem):
+    small = (
+        pltpu.make_async_copy(summed, out_sum, sem.at[1]),
+        pltpu.make_async_copy(scales, out_scales, sem.at[2]),
+    )
+    for copy in small:
+        copy.start()
+
+    def put(p, carry):
+        pltpu.make_async_copy(arr.at[src[0, p]], out.at[p], sem.at[0]).start()
+        return carry
+
+    lax.fori_loop(0, 64, put, 0, unroll=8)
+    for copy in small:
+        copy.wait()
+    pltpu.make_async_copy(arr, out, sem.at[0]).wait()
 
 
 def per_device(queries, cache_pool, block_scale, block_table, lengths, output_weight):
-    y = lax.axis_index("seq")
-    g = lax.axis_index("grp")
-    me = y * NGRP + g
-    table = block_table.reshape(NGRP, 2, NSEQ, 32).transpose(2, 0, 1, 3).reshape(NDEV, 64)
-    spot = jnp.arange(64, dtype=jnp.int32)[None]
-    code = (table % 64) * 64 + spot
-    mine = table // 64 == me
-    low = jnp.min(jnp.where(mine, code, 1 << 20), axis=1)
-    high = jnp.max(jnp.where(mine, code, -1), axis=1)
-    codes = jnp.stack([low, high], axis=1)
-    slots = codes // 64
-    second = codes % 64 // 32
-    column = (jnp.arange(NDEV, dtype=jnp.int32) // NGRP)[:, None] * 32 + codes % 32
-    pairs = jnp.tile(lengths.reshape(NGRP, 2), (NSEQ, 1))
-    length = jnp.where(second == 0, pairs[:, :1], pairs[:, 1:])
-    limit = jnp.clip(length - column * BLK, 0, BLK)
-    idx = jnp.concatenate([
-        slots.reshape(-1),
-        jnp.where(second == 0, limit, 0).reshape(-1),
-        jnp.where(second == 1, limit, 0).reshape(-1),
-    ])
-    chosen = slots.reshape(-1)[:, None] == jnp.arange(64, dtype=jnp.int32)[None]
-    scales = block_scale.reshape(64, 2).astype(jnp.float32)
-    scal = jnp.sum(jnp.where(chosen[None], scales.T[:, None, :], 0.0), axis=2).reshape(-1)
-    own = lax.dynamic_slice(block_table, (2 * g, 32 * y), (2, 32)).reshape(64)
-    before = (own[None, :] // 64 == own[:, None] // 64) & (own[None, :] < own[:, None])
-    place = (own // 64) * 2 + jnp.sum(before.astype(jnp.int32), axis=1)
-
     vmem = pl.BlockSpec(memory_space=pltpu.VMEM)
     smem = pl.BlockSpec(memory_space=pltpu.SMEM)
-    hbm = pl.BlockSpec(memory_space=pl.ANY)
+    hbm = pl.BlockSpec(memory_space=pltpu.HBM)
+    anywhere = pl.BlockSpec(memory_space=pl.ANY)
     dma = pltpu.SemaphoreType.DMA
-    arrived, summed, decode_scale = pl.pallas_call(
+    arrived, summed, scales, place = pl.pallas_call(
         exchange_kernel,
         out_shape=(
             jax.ShapeDtypeStruct((NDEV, 512, BLK), jnp.bfloat16),
             jax.ShapeDtypeStruct((2, 256), jnp.bfloat16),
-            jax.ShapeDtypeStruct((64, 2), jnp.bfloat16),
+            jax.ShapeDtypeStruct((2, 2, 32), jnp.bfloat16),
+            jax.ShapeDtypeStruct((1, BLK), jnp.int32),
         ),
-        in_specs=[smem, smem, hbm, vmem, hbm, vmem],
-        out_specs=(vmem, vmem, vmem),
+        in_specs=[hbm] * 6,
+        out_specs=(vmem, vmem, vmem, vmem),
         scratch_shapes=[
+            pltpu.VMEM((16, BLK), jnp.int32),
+            pltpu.VMEM((2, 64), jnp.bfloat16),
+            pltpu.VMEM((16, BLK), jnp.int32),
+            pltpu.VMEM((2, 64), jnp.float32),
+            pltpu.SMEM((16, BLK), jnp.int32),
+            pltpu.SMEM((2, 64), jnp.float32),
+            pltpu.SMEM((16,), jnp.int32),
             pltpu.VMEM((64, BLK, BLK), jnp.bfloat16),
             pltpu.VMEM((64, BLK, BLK), jnp.bfloat16),
             pltpu.VMEM((NDEV, 512, BLK), jnp.bfloat16),
+            pltpu.VMEM((16, BLK), jnp.bfloat16),
             pltpu.VMEM((NGRP, 16, BLK), jnp.bfloat16),
             pltpu.VMEM((1024, 256), jnp.bfloat16),
             pltpu.VMEM((NDEV, 8, BLK), jnp.float32),
@@ -289,26 +326,37 @@
             pltpu.VMEM((NDEV, 4, BLK), jnp.float32),
             pltpu.VMEM((NTP, 2, 256), jnp.float32),
             pltpu.VMEM((NTP, 2, 256), jnp.float32),
-            dma((2,)), dma, dma((NGRP,)), dma((NGRP,)),
+            dma((9,)), dma((NGRP,)), dma((NGRP,)),
             dma((4, NDEV)), dma((4, NDEV)),
             dma((NDEV,)), dma((NDEV,)), dma((NDEV,)), dma((NDEV,)),
             dma((NTP,)), dma((NTP,)),
         ],
-        compiler_params=pltpu.CompilerParams(collective_id=0, has_side_effects=True),
-    )(
-        idx, scal, cache_pool.reshape(64, 256, BLK), queries.reshape(16, BLK), output_weight, place[:, None],
-    )
-    decode_cache = pl.pallas_call(
+        compiler_params=pltpu.CompilerParams(
+            collective_id=0, has_side_effects=True, vmem_limit_bytes=24 << 20
+        ),
+    )(*(
+        pltpu.with_memory_space_constraint(operand, pltpu.HBM)
+        for operand in (
+            block_table, lengths, block_scale.reshape(64, 2).T, cache_pool.reshape(64, 256, BLK),
+            queries.reshape(16, BLK), output_weight,
+        )
+    ))
+    decode_cache, attention_output, decode_scale = pl.pallas_call(
         place_kernel,
-        out_shape=jax.ShapeDtypeStruct((64, 256, BLK), jnp.bfloat16),
-        in_specs=[smem, vmem],
-        out_specs=hbm,
-        scratch_shapes=[dma],
-    )(place, arrived.reshape(64, 256, BLK))
+        out_shape=(
+            jax.ShapeDtypeStruct((64, 256, BLK), jnp.bfloat16),
+            jax.ShapeDtypeStruct((2, 256), jnp.bfloat16),
+            jax.ShapeDtypeStruct((2, 2, 32), jnp.bfloat16),
+        ),
+        in_specs=[smem, vmem, vmem, vmem],
+        out_specs=(hbm, hbm, hbm),
+        scratch_shapes=[dma((3,))],
+        compiler_params=pltpu.CompilerParams(vmem_limit_bytes=12 << 20),
+    )(place, arrived.reshape(64, 256, BLK), summed, scales)
     return (
-        summed,
+        attention_output,
         decode_cache.reshape(2, 32, 1, 2, BLK, BLK),
-        decode_scale.reshape(2, 32, 1, 2),
+        decode_scale.transpose(0, 2, 1).reshape(2, 32, 1, 2),
     )
 
 

time: 82.2 us -> 68.8 us (0.84)
  local copies, waits for them, and re-layouts: 5.64 us -> 0 us
  Pallas kernels: 72.2 us -> 68.1 us
  other arithmetic: 3.32 us -> 0 us
    pallas_call x1, Pallas kernels: 68 us -> 65.5 us  [per_device(): pl.pallas_call(exchange_kernel, out_shape=(jax.ShapeDtypeStruct((NDEV, 51...]
    pallas_call x1, Pallas kernels: 4.17 us -> 2.53 us  [per_device(): pl.pallas_call(place_kernel, out_shape=(jax.ShapeDtypeStruct((64, 256, BL...]
    reshape x3 -> x0, local copies, waits for them, and re-layouts: 1.49 us -> none  [the longest x1 0.78 us: per_device(): block_table.reshape(NGRP, 2, NSEQ, 32).transpose(2, 0, 1, 3)]
    another operation x9 -> x0, local copies, waits for them, and re-layouts: 1.36 us -> none  [the longest x4 0.9 us: per_device(): pairs = jnp.tile(lengths.reshape(NGRP, 2), (NSEQ, 1))]
    add x3 -> x0, other arithmetic: 1.25 us -> none  [the longest x2 1.25 us: per_device(): place = own // 64 * 2 + jnp.sum(before.astype(jnp.int32), axis=1)]
    unnamed x6 -> x0, local copies, waits for them, and re-layouts: 1.23 us -> none
where the time goes in v2:
time: 68.8 us; the launch traced here: 68.7 us
  Pallas kernels  68.1 us (99%)
    pallas_call x1, Pallas kernels, per_device(): pl.pallas_call(exchange_kernel, out_shape=(jax.ShapeDtypeStruct((NDEV, 51...  65.5 us
    pallas_call x1, Pallas kernels, per_device(): pl.pallas_call(place_kernel, out_shape=(jax.ShapeDtypeStruct((64, 256, BL...  2.53 us

profile of v2, /device:TPU:1, one launch (start us, length us, event | category | flops | bytes accessed | tf_op | source)
XLA Modules:
  0.0 68.7 jit_solution(9452725356436226393)
XLA Ops:
  0.6 65.5 %shard_map.85 = (bf16[32,512,128]{2,1,0:T(8,128)(2,1)S(1)}, bf16[2,256]{1,0:T(2,128)(2,1)S(1)}, bf16[2,2,32]{2,1,0:T(2,128)(2,1)S(1)}, s32[1,128]{1,0:T(1,128)S(1)}) custom-call(s32[16,128]{1,0:T(8,128)} %table_hbm.1, s32[16]{0:T(128)} %lengths_hbm.1, bf16[2,64]{1,0:T(2,128)(2,1)} %bitcast.15, bf16[64,256,128]{2,1,0:T(8,128)(2,1)} %bitcast.13, ...), custom_call_target="tpu_custom_call" | custom-call | tf_op jit(solution)/shard_map/pallas_call | solution.py:299
  66.2 2.5 %shard_map.86 = (bf16[64,256,128]{2,1,0:T(8,128)(2,1)}, bf16[2,256]{1,0:T(2,128)(2,1)}, bf16[2,2,32]{2,1,0:T(2,128)(2,1)}) custom-call(s32[1,128]{1,0:T(1,128)S(1)} %get-tuple-element.10.src, bf16[64,256,128]{2,1,0:T(8,128)(2,1)S(1)} %bitcast.12, bf16[2,256]{1,0:T(2,128)(2,1)S(1)} %get-tuple-element.12.summed, bf16[2,2,32]{2,1,0:T(2,128)(2,1)S(1)} %get-tuple-element.13.scales), custom_call_target="tpu_custom_call" | custom-call | tf_op jit(solution)/shard_map/pallas_call | solution.py:344

commit v3 on v2

--- a/solution.py
+++ b/solution.py
@@ -17,10 +17,11 @@
 START = (0, 256, 128, 384)
 
 
-def spread(i):
-    turn, rest = i // 8, i % 8
-    dy, dc = rest // 2, rest % 2
-    return dy, (dy + turn) % 4, dc
+PEERS = [
+    (dy, (dy + turn) % 4, dc)
+    for turn in range(4) for dy in range(4) for dc in range(2)
+    if (dy, turn, dc) != (0, 0, 0)
+]
 
 
 def exchange_kernel(
@@ -28,18 +29,20 @@
     arr, out_ref, scale_out, place_out,
     table, scale_in, codes_v, scales_v, codes, scal, lens,
     pool_k, pool_v, send, q_ref, qall, w, pmsg, part, amsg, att, pout, zbuf,
-    in_sem, q_ssem, q_rsem, b_ssem, b_rsem, p_ssem, p_rsem, a_ssem, a_rsem, z_ssem, z_rsem,
+    in_sem, q_sem, b_sem, p_sem, a_sem, z_sem,
 ):
     y = lax.axis_index("seq")
     z = lax.axis_index("tp")
     g = lax.axis_index("grp")
     me = y * NGRP + g
 
-    def peer(i):
-        dy, dx, dc = spread(i)
-        ty = (y + dy) % 4
-        tg = ((g // 2 + dx) % 4) * 2 + (g + dc) % 2
-        return ty, tg
+    ys = [(y + k) % NSEQ for k in range(NSEQ)]
+    xs = [((g // 2 + k) % 4) * 2 for k in range(4)]
+    cs = [(g + k) % 2 for k in range(2)]
+
+    def peer(offset):
+        dy, dx, dc = offset
+        return ys[dy], xs[dx] + cs[dc]
 
     table_in = pltpu.make_async_copy(table_hbm, table, in_sem.at[0])
     keys_in = pltpu.make_async_copy(pool_hbm.at[:, pl.ds(0, BLK)], pool_k, in_sem.at[1])
@@ -54,19 +57,11 @@
         copy.start()
 
     barrier = pltpu.get_barrier_semaphore()
-
-    def greet(i, carry):
-        ty, tg = peer(i)
+    for offset in PEERS:
+        ty, tg = peer(offset)
         pl.semaphore_signal(barrier, inc=1, device_id={"seq": ty, "grp": tg}, device_id_type=MESH)
-        return carry
-
-    lax.fori_loop(1, NDEV, greet, 0)
-
-    def greet_z(i, carry):
-        pl.semaphore_signal(barrier, inc=1, device_id={"tp": (z + i) % NTP}, device_id_type=MESH)
-        return carry
-
-    lax.fori_loop(1, NTP, greet_z, 0)
+    for k in range(1, NTP):
+        pl.semaphore_signal(barrier, inc=1, device_id={"tp": (z + k) % NTP}, device_id_type=MESH)
 
     row16 = lax.broadcasted_iota(jnp.int32, (16, BLK), 0)
     lane16 = lax.broadcasted_iota(jnp.int32, (16, BLK), 1)
@@ -105,37 +100,31 @@
 
         lax.fori_loop(0, NDEV, body, 0)
 
-    def block_copy(c, i):
-        ty, tg = peer(i)
+    def remote(src, dst, sems, device):
+        return pltpu.make_async_remote_copy(
+            src_ref=src, dst_ref=dst, send_sem=sems.at[0], recv_sem=sems.at[1],
+            device_id=device, device_id_type=MESH,
+        )
+
+    def send_wave(c):
         rows = pl.ds(START[c], BLK)
-        return pltpu.make_async_remote_copy(
-            src_ref=send.at[ty * NGRP + tg, rows],
-            dst_ref=arr.at[me, rows],
-            send_sem=b_ssem.at[c, i],
-            recv_sem=b_rsem.at[c, i],
-            device_id={"seq": ty, "grp": tg},
-            device_id_type=MESH,
-        )
-
-    def send_wave(c):
-        def body(i, carry):
-            block_copy(c, i).start()
-            return carry
-
-        lax.fori_loop(1, NDEV, body, 0)
-
-    def q_copy(i):
-        tg = (g + i) % NGRP
-        return pltpu.make_async_remote_copy(
-            src_ref=q_ref, dst_ref=qall.at[g], send_sem=q_ssem.at[i], recv_sem=q_rsem.at[i],
-            device_id={"grp": tg}, device_id_type=MESH,
-        )
+        for offset in PEERS:
+            ty, tg = peer(offset)
+            remote(send.at[ty * NGRP + tg, rows], arr.at[me, rows], b_sem, {"seq": ty, "grp": tg}).start()
+
+    here = {"seq": ys[1]}
+    rest = pl.ds(0, NDEV - 1)
+    q_all = remote(qall.at[pl.ds(0, NGRP - 1)], qall.at[pl.ds(0, NGRP - 1)], q_sem, here)
+    b_all = remote(send.at[rest], arr.at[rest], b_sem, here)
+    p_all = remote(pmsg.at[rest], part.at[rest], p_sem, here)
+    a_all = remote(att.at[rest], att.at[rest], a_sem, here)
+    z_all = remote(pout.at[pl.ds(0, NTP - 1)], zbuf.at[pl.ds(0, NTP - 1)], z_sem, here)
 
     keys_in.wait()
     pick(0)
     pl.semaphore_wait(barrier, NDEV - 1 + NTP - 1)
-    for i in range(1, NGRP):
-        q_copy(i).start()
+    for k in range(1, NGRP):
+        remote(q_ref, qall.at[g], q_sem, {"grp": (g + k) % NGRP}).start()
     send_wave(0)
     pick(1)
     vals_in.wait()
@@ -143,8 +132,7 @@
     pick(3)
     scales_out.wait()
     lens_in.wait()
-    for i in range(1, NGRP):
-        q_copy(i).wait()
+    q_all.wait_recv()
 
     row4 = lax.broadcasted_iota(jnp.int32, (4, BLK), 0)
     lane4 = lax.broadcasted_iota(jnp.int32, (4, BLK), 1)
@@ -189,33 +177,12 @@
 
     lax.fori_loop(0, NGRP, attend, 0)
 
-    def p_copy(i):
-        ty, tg = peer(i)
-        return pltpu.make_async_remote_copy(
-            src_ref=pmsg.at[ty * NGRP + tg], dst_ref=part.at[me],
-            send_sem=p_ssem.at[i], recv_sem=p_rsem.at[i],
-            device_id={"seq": ty, "grp": tg}, device_id_type=MESH,
-        )
-
-    def a_copy(i):
-        ty, tg = peer(i)
-        return pltpu.make_async_remote_copy(
-            src_ref=amsg, dst_ref=att.at[(y % 2) * 16 + g * 2 + y // 2],
-            send_sem=a_ssem.at[i], recv_sem=a_rsem.at[i],
-            device_id={"seq": ty, "grp": tg}, device_id_type=MESH,
-        )
-
-    def each(make, what, first, last):
-        def body(i, carry):
-            getattr(make(i), what)()
-            return carry
-
-        lax.fori_loop(first, last, body, 0)
-
-    each(p_copy, "start", 1, NDEV)
+    for offset in PEERS:
+        ty, tg = peer(offset)
+        remote(pmsg.at[ty * NGRP + tg], part.at[me], p_sem, {"seq": ty, "grp": tg}).start()
     part[me] = pmsg[me]
     send_wave(1)
-    each(p_copy, "wait", 1, NDEV)
+    p_all.wait_recv()
 
     peaks = part[:, pl.ds(4, 4), 2:3]
     sums = part[:, pl.ds(4, 4), 3:4]
@@ -226,7 +193,9 @@
     rows = (numer / denom).astype(jnp.bfloat16).astype(jnp.float32)
     amsg[...] = rows
     att[(y % 2) * 16 + g * 2 + y // 2] = rows
-    each(a_copy, "start", 1, NDEV)
+    for offset in PEERS:
+        ty, tg = peer(offset)
+        remote(amsg, att.at[(y % 2) * 16 + g * 2 + y // 2], a_sem, {"seq": ty, "grp": tg}).start()
     send_wave(2)
     send_wave(3)
     arr[me] = send[me]
@@ -247,7 +216,7 @@
     scale_out[0] = picked[0:2, 0:32]
     scale_out[1] = picked[0:2, 32:64]
     w_in.wait()
-    each(a_copy, "wait", 1, NDEV)
+    a_all.wait_recv()
 
     total = jnp.zeros((16, 256), jnp.float32)
     for h in range(8):
@@ -256,20 +225,16 @@
     for k in range(NTP):
         pout[k] = total[2 * k : 2 * k + 2]
 
-    def z_copy(i):
-        tz = (z + i) % NTP
-        return pltpu.make_async_remote_copy(
-            src_ref=pout.at[tz], dst_ref=zbuf.at[z], send_sem=z_ssem.at[i], recv_sem=z_rsem.at[i],
-            device_id={"tp": tz}, device_id_type=MESH,
-        )
-
-    each(z_copy, "start", 1, NTP)
+    for k in range(1, NTP):
+        tz = (z + k) % NTP
+        remote(pout.at[tz], zbuf.at[z], z_sem, {"tp": tz}).start()
     zbuf[z] = pout[z]
-    each(z_copy, "wait", 1, NTP)
+    z_all.wait_recv()
     out_ref[...] = jnp.sum(zbuf[...], axis=0).astype(jnp.bfloat16)
 
-    for c in range(4):
-        each(functools.partial(block_copy, c), "wait", 1, NDEV)
+    for phase in (q_all, p_all, a_all, z_all, b_all):
+        phase.wait_send()
+    b_all.wait_recv()
 
 
 def place_kernel(src, arr, summed, scales, out, out_sum, out_scales, sem):
@@ -326,10 +291,7 @@
             pltpu.VMEM((NDEV, 4, BLK), jnp.float32),
             pltpu.VMEM((NTP, 2, 256), jnp.float32),
             pltpu.VMEM((NTP, 2, 256), jnp.float32),
-            dma((9,)), dma((NGRP,)), dma((NGRP,)),
-            dma((4, NDEV)), dma((4, NDEV)),
-            dma((NDEV,)), dma((NDEV,)), dma((NDEV,)), dma((NDEV,)),
-            dma((NTP,)), dma((NTP,)),
+            dma((9,)), dma((2,)), dma((2,)), dma((2,)), dma((2,)), dma((2,)),
         ],
         compiler_params=pltpu.CompilerParams(
             collective_id=0, has_side_effects=True, vmem_limit_bytes=24 << 20

time: 68.8 us -> 64.4 us (0.936)
  Pallas kernels: 68.1 us -> 63.7 us
    pallas_call x1, Pallas kernels: 65.5 us -> 61.1 us  [per_device(): pl.pallas_call(exchange_kernel, out_shape=(jax.ShapeDtypeStruct((NDEV, 51...]
where the time goes in v3:
time: 64.4 us; the launch traced here: 64.3 us
  Pallas kernels  63.7 us (99%)
    pallas_call x1, Pallas kernels, per_device(): pl.pallas_call(exchange_kernel, out_shape=(jax.ShapeDtypeStruct((NDEV, 51...  61.1 us
    pallas_call x1, Pallas kernels, per_device(): pl.pallas_call(place_kernel, out_shape=(jax.ShapeDtypeStruct((64, 256, BL...  2.53 us

profile of v3, /device:TPU:1, one launch (start us, length us, event | category | flops | bytes accessed | tf_op | source)
XLA Modules:
  0.0 64.3 jit_solution(2483562920870657164)
XLA Ops:
  0.6 61.1 %shard_map.85 = (bf16[32,512,128]{2,1,0:T(8,128)(2,1)S(1)}, bf16[2,256]{1,0:T(2,128)(2,1)S(1)}, bf16[2,2,32]{2,1,0:T(2,128)(2,1)S(1)}, s32[1,128]{1,0:T(1,128)S(1)}) custom-call(s32[16,128]{1,0:T(8,128)} %table_hbm.1, s32[16]{0:T(128)} %lengths_hbm.1, bf16[2,64]{1,0:T(2,128)(2,1)} %bitcast.15, bf16[64,256,128]{2,1,0:T(8,128)(2,1)} %bitcast.13, ...), custom_call_target="tpu_custom_call" | custom-call | tf_op jit(solution)/shard_map/pallas_call | solution.py:264
  61.8 2.5 %shard_map.86 = (bf16[64,256,128]{2,1,0:T(8,128)(2,1)}, bf16[2,256]{1,0:T(2,128)(2,1)}, bf16[2,2,32]{2,1,0:T(2,128)(2,1)}) custom-call(s32[1,128]{1,0:T(1,128)S(1)} %get-tuple-element.10.src, bf16[64,256,128]{2,1,0:T(8,128)(2,1)S(1)} %bitcast.12, bf16[2,256]{1,0:T(2,128)(2,1)S(1)} %get-tuple-element.12.summed, bf16[2,2,32]{2,1,0:T(2,128)(2,1)S(1)} %get-tuple-element.13.scales), custom_call_target="tpu_custom_call" | custom-call | tf_op jit(solution)/shard_map/pallas_call | solution.py:306

commit v4 on v3

--- a/solution.py
+++ b/solution.py
@@ -28,8 +28,8 @@
     table_hbm, lengths_hbm, scale_hbm, pool_hbm, q_hbm, w_hbm,
     arr, out_ref, scale_out, place_out,
     table, scale_in, codes_v, scales_v, codes, scal, lens,
-    pool_k, pool_v, send, q_ref, qall, w, pmsg, part, amsg, att, pout, zbuf,
-    in_sem, q_sem, b_sem, p_sem, a_sem, z_sem,
+    pool_k, pool_v, send, q_ref, qall, w, pmsg, part, smsg, stat, amsg, att, attended, pout, zbuf,
+    in_sem, q_sem, b_sem, p_sem, s_sem, a_sem, z_sem,
 ):
     y = lax.axis_index("seq")
     z = lax.axis_index("tp")
@@ -90,6 +90,11 @@
     def code_of(q, gg, r):
         return codes[2 * gg, q + 4 * r]
 
+    def pick_one(c, ty, tg):
+        pool, r = (pool_k, pool_v)[c // 2], c % 2
+        slot = (code_of(ty, tg, r) >> 6) & 63
+        send[ty * NGRP + tg, pl.ds(START[c], BLK), :] = pool[slot]
+
     def pick(c):
         pool, r = (pool_k, pool_v)[c // 2], c % 2
 
@@ -117,15 +122,18 @@
     q_all = remote(qall.at[pl.ds(0, NGRP - 1)], qall.at[pl.ds(0, NGRP - 1)], q_sem, here)
     b_all = remote(send.at[rest], arr.at[rest], b_sem, here)
     p_all = remote(pmsg.at[rest], part.at[rest], p_sem, here)
+    s_all = remote(stat.at[rest], stat.at[rest], s_sem, here)
     a_all = remote(att.at[rest], att.at[rest], a_sem, here)
     z_all = remote(pout.at[pl.ds(0, NTP - 1)], zbuf.at[pl.ds(0, NTP - 1)], z_sem, here)
 
     keys_in.wait()
-    pick(0)
+    for offset in PEERS:
+        pick_one(0, *peer(offset))
     pl.semaphore_wait(barrier, NDEV - 1 + NTP - 1)
     for k in range(1, NGRP):
         remote(q_ref, qall.at[g], q_sem, {"grp": (g + k) % NGRP}).start()
     send_wave(0)
+    pick_one(0, y, g)
     pick(1)
     vals_in.wait()
     pick(2)
@@ -134,8 +142,7 @@
     lens_in.wait()
     q_all.wait_recv()
 
-    row4 = lax.broadcasted_iota(jnp.int32, (4, BLK), 0)
-    lane4 = lax.broadcasted_iota(jnp.int32, (4, BLK), 1)
+    lane1 = lax.broadcasted_iota(jnp.int32, (1, BLK), 1)
 
     def attend(gg, carry):
         q = qall[gg]
@@ -164,35 +171,41 @@
             scaled = (weight * value_scales[n]).astype(jnp.bfloat16)
             acc = acc + jnp.dot(scaled, send[t, pl.ds(r * 256 + BLK, BLK), :], preferred_element_type=jnp.float32)
         denom = jnp.sum(total, axis=1, keepdims=True)
-        stats = jnp.where(lane16 == 2, peak, jnp.where(lane16 == 3, denom, 0.0))
+        line = jnp.where(lane16 == row16, peak, jnp.where(lane16 == row16 + 16, denom, 0.0))
+        line = jnp.sum(line, axis=0, keepdims=True)
+        for n in range(8):
+            line = jnp.where(lane1 == 32 + 2 * n, key_scales[n], line)
+            line = jnp.where(lane1 == 33 + 2 * n, value_scales[n], line)
+        smsg[gg] = line
         for qq in range(NSEQ):
-            t = qq * NGRP + gg
-            pmsg[t, pl.ds(0, 4), :] = acc[4 * qq : 4 * qq + 4]
-            low = stats[4 * qq : 4 * qq + 4]
-            for r in range(2):
-                low = jnp.where((row4 == r) & (lane4 == 0), key_scales[2 * qq + r], low)
-                low = jnp.where((row4 == r) & (lane4 == 1), value_scales[2 * qq + r], low)
-            pmsg[t, pl.ds(4, 4), :] = low
+            pmsg[qq * NGRP + gg] = acc[4 * qq : 4 * qq + 4].astype(jnp.bfloat16)
         return carry
 
     lax.fori_loop(0, NGRP, attend, 0)
 
     for offset in PEERS:
         ty, tg = peer(offset)
+        remote(smsg.at[tg], stat.at[me], s_sem, {"seq": ty, "grp": tg}).start()
         remote(pmsg.at[ty * NGRP + tg], part.at[me], p_sem, {"seq": ty, "grp": tg}).start()
     part[me] = pmsg[me]
+    stat[me] = smsg[g]
     send_wave(1)
+    s_all.wait_recv()
     p_all.wait_recv()
 
-    peaks = part[:, pl.ds(4, 4), 2:3]
-    sums = part[:, pl.ds(4, 4), 3:4]
+    lines = jnp.broadcast_to(stat[...], (NDEV, 4, BLK))
+    row = lax.broadcasted_iota(jnp.int32, (NDEV, 4, BLK), 1) + 4 * y
+    lane = lax.broadcasted_iota(jnp.int32, (NDEV, 4, BLK), 2)
+    peaks = jnp.sum(jnp.where(lane == row, lines, 0.0), axis=2, keepdims=True)
+    sums = jnp.sum(jnp.where(lane == row + 16, lines, 0.0), axis=2, keepdims=True)
     peak = jnp.max(peaks, axis=0, keepdims=True)
     factor = jnp.exp(peaks - peak)
     denom = jnp.sum(sums * factor, axis=0)
-    numer = jnp.sum(part[:, pl.ds(0, 4), :] * factor, axis=0)
-    rows = (numer / denom).astype(jnp.bfloat16).astype(jnp.float32)
+    numer = jnp.sum(part[...].astype(jnp.float32) * factor, axis=0)
+    rows = (numer / denom).astype(jnp.bfloat16)
     amsg[...] = rows
     att[(y % 2) * 16 + g * 2 + y // 2] = rows
+
     for offset in PEERS:
         ty, tg = peer(offset)
         remote(amsg, att.at[(y % 2) * 16 + g * 2 + y // 2], a_sem, {"seq": ty, "grp": tg}).start()
@@ -209,18 +222,23 @@
     before = inside & ((down >> 6) == (across >> 6)) & (down < across)
     rank = jnp.sum(before.astype(jnp.int32), axis=0, keepdims=True)
     place_out[...] = ((own >> 6) * 2 + rank) & 63
-    lines = lax.broadcasted_iota(jnp.int32, (256, BLK), 0)
-    hot = (lines == (own >> 6) * 8 + 4 + rank).astype(jnp.float32).astype(jnp.bfloat16)
-    flat = part[...].reshape(256, BLK).T[0:8].astype(jnp.bfloat16)
-    picked = jnp.dot(flat, hot, preferred_element_type=jnp.float32).astype(jnp.bfloat16)
-    scale_out[0] = picked[0:2, 0:32]
-    scale_out[1] = picked[0:2, 32:64]
+    owner = lax.broadcasted_iota(jnp.int32, (NDEV, BLK), 0)
+    hot = (owner == (own >> 6)).astype(jnp.float32).astype(jnp.bfloat16)
+    flat = stat[...].reshape(NDEV, BLK).T.astype(jnp.bfloat16)
+    picked = jnp.dot(flat, hot, preferred_element_type=jnp.float32)
+    depth = lax.broadcasted_iota(jnp.int32, (BLK, BLK), 0)
+    for kv in range(2):
+        line = jnp.where(depth == 32 + 4 * y + 2 * rank + kv, picked, 0.0)
+        line = jnp.sum(line, axis=0, keepdims=True).astype(jnp.bfloat16)
+        scale_out[0, kv : kv + 1, :] = line[:, 0:32]
+        scale_out[1, kv : kv + 1, :] = line[:, 32:64]
     w_in.wait()
     a_all.wait_recv()
+    attended[...] = att[...].astype(jnp.float32)
 
     total = jnp.zeros((16, 256), jnp.float32)
     for h in range(8):
-        lhs = att[pl.ds((h // 4) * 16, 16), h % 4, :].astype(jnp.bfloat16)
+        lhs = attended[pl.ds((h // 4) * 16, 16), h % 4, :].astype(jnp.bfloat16)
         total = total + jnp.dot(lhs, w[pl.ds(h * BLK, BLK), :], preferred_element_type=jnp.float32)
     for k in range(NTP):
         pout[k] = total[2 * k : 2 * k + 2]
@@ -232,7 +250,7 @@
     z_all.wait_recv()
     out_ref[...] = jnp.sum(zbuf[...], axis=0).astype(jnp.bfloat16)
 
-    for phase in (q_all, p_all, a_all, z_all, b_all):
+    for phase in (q_all, s_all, p_all, a_all, z_all, b_all):
         phase.wait_send()
     b_all.wait_recv()
 
@@ -285,13 +303,16 @@
             pltpu.VMEM((16, BLK), jnp.bfloat16),
             pltpu.VMEM((NGRP, 16, BLK), jnp.bfloat16),
             pltpu.VMEM((1024, 256), jnp.bfloat16),
-            pltpu.VMEM((NDEV, 8, BLK), jnp.float32),
-            pltpu.VMEM((NDEV, 8, BLK), jnp.float32),
-            pltpu.VMEM((4, BLK), jnp.float32),
+            pltpu.VMEM((NDEV, 4, BLK), jnp.bfloat16),
+            pltpu.VMEM((NDEV, 4, BLK), jnp.bfloat16),
+            pltpu.VMEM((NGRP, 1, BLK), jnp.float32),
+            pltpu.VMEM((NDEV, 1, BLK), jnp.float32),
+            pltpu.VMEM((4, BLK), jnp.bfloat16),
+            pltpu.VMEM((NDEV, 4, BLK), jnp.bfloat16),
             pltpu.VMEM((NDEV, 4, BLK), jnp.float32),
             pltpu.VMEM((NTP, 2, 256), jnp.float32),
             pltpu.VMEM((NTP, 2, 256), jnp.float32),
-            dma((9,)), dma((2,)), dma((2,)), dma((2,)), dma((2,)), dma((2,)),
+            dma((9,)), dma((2,)), dma((2,)), dma((2,)), dma((2,)), dma((2,)), dma((2,)),
         ],
         compiler_params=pltpu.CompilerParams(
             collective_id=0, has_side_effects=True, vmem_limit_bytes=24 << 20

time: 64.4 us -> 63.2 us (0.981)
  Pallas kernels: 63.7 us -> 62.5 us
    pallas_call x1, Pallas kernels: 61.1 us -> 59.9 us  [per_device(): pl.pallas_call(exchange_kernel, out_shape=(jax.ShapeDtypeStruct((NDEV, 51...]
where the time goes in v4:
time: 63.2 us; the launch traced here: 63.1 us
  Pallas kernels  62.5 us (99%)
  between operations  0.64 us (1%)
    pallas_call x1, Pallas kernels, per_device(): pl.pallas_call(exchange_kernel, out_shape=(jax.ShapeDtypeStruct((NDEV, 51...  59.9 us
    pallas_call x1, Pallas kernels, per_device(): pl.pallas_call(place_kernel, out_shape=(jax.ShapeDtypeStruct((64, 256, BL...  2.53 us

profile of v4, /device:TPU:1, one launch (start us, length us, event | category | flops | bytes accessed | tf_op | source)
XLA Modules:
  0.0 63.1 jit_solution(3782959417189671927)
XLA Ops:
  0.6 59.9 %shard_map.85 = (bf16[32,512,128]{2,1,0:T(8,128)(2,1)S(1)}, bf16[2,256]{1,0:T(2,128)(2,1)S(1)}, bf16[2,2,32]{2,1,0:T(2,128)(2,1)S(1)}, s32[1,128]{1,0:T(1,128)S(1)}) custom-call(s32[16,128]{1,0:T(8,128)} %table_hbm.1, s32[16]{0:T(128)} %lengths_hbm.1, bf16[2,64]{1,0:T(2,128)(2,1)} %bitcast.15, bf16[64,256,128]{2,1,0:T(8,128)(2,1)} %bitcast.13, ...), custom_call_target="tpu_custom_call" | custom-call | tf_op jit(solution)/shard_map/pallas_call | solution.py:282
  60.6 2.5 %shard_map.86 = (bf16[64,256,128]{2,1,0:T(8,128)(2,1)}, bf16[2,256]{1,0:T(2,128)(2,1)}, bf16[2,2,32]{2,1,0:T(2,128)(2,1)}) custom-call(s32[1,128]{1,0:T(1,128)S(1)} %get-tuple-element.10.src, bf16[64,256,128]{2,1,0:T(8,128)(2,1)S(1)} %bitcast.12, bf16[2,256]{1,0:T(2,128)(2,1)S(1)} %get-tuple-element.12.summed, bf16[2,2,32]{2,1,0:T(2,128)(2,1)S(1)} %get-tuple-element.13.scales), custom_call_target="tpu_custom_call" | custom-call | tf_op jit(solution)/shard_map/pallas_call | solution.py:327

commit v5 on v4

--- a/solution.py
+++ b/solution.py
@@ -29,7 +29,7 @@
     arr, out_ref, scale_out, place_out,
     table, scale_in, codes_v, scales_v, codes, scal, lens,
     pool_k, pool_v, send, q_ref, qall, w, pmsg, part, smsg, stat, amsg, att, attended, pout, zbuf,
-    in_sem, q_sem, b_sem, p_sem, s_sem, a_sem, z_sem,
+    climb, descend, in_sem, q_sem, b_sem, p_sem, s_sem, a_sem, z_sem,
 ):
     y = lax.axis_index("seq")
     z = lax.axis_index("tp")
@@ -60,8 +60,15 @@
     for offset in PEERS:
         ty, tg = peer(offset)
         pl.semaphore_signal(barrier, inc=1, device_id={"seq": ty, "grp": tg}, device_id_type=MESH)
-    for k in range(1, NTP):
-        pl.semaphore_signal(barrier, inc=1, device_id={"tp": (z + k) % NTP}, device_id_type=MESH)
+    above, below = z < NTP - 1, z > 0
+
+    @pl.when(above)
+    def _():
+        pl.semaphore_signal(barrier, inc=1, device_id={"tp": z + 1}, device_id_type=MESH)
+
+    @pl.when(below)
+    def _():
+        pl.semaphore_signal(barrier, inc=1, device_id={"tp": z - 1}, device_id_type=MESH)
 
     row16 = lax.broadcasted_iota(jnp.int32, (16, BLK), 0)
     lane16 = lax.broadcasted_iota(jnp.int32, (16, BLK), 1)
@@ -129,7 +136,7 @@
     keys_in.wait()
     for offset in PEERS:
         pick_one(0, *peer(offset))
-    pl.semaphore_wait(barrier, NDEV - 1 + NTP - 1)
+    pl.semaphore_wait(barrier, NDEV - 1 + jnp.where(above, 1, 0) + jnp.where(below, 1, 0))
     for k in range(1, NGRP):
         remote(q_ref, qall.at[g], q_sem, {"grp": (g + k) % NGRP}).start()
     send_wave(0)
@@ -232,6 +239,19 @@
         line = jnp.sum(line, axis=0, keepdims=True).astype(jnp.bfloat16)
         scale_out[0, kv : kv + 1, :] = line[:, 0:32]
         scale_out[1, kv : kv + 1, :] = line[:, 32:64]
+    @pl.when(below)
+    def _():
+        pl.semaphore_wait(climb, 1)
+
+    @pl.when(above)
+    def _():
+        pl.semaphore_signal(climb, inc=1, device_id={"tp": z + 1}, device_id_type=MESH)
+        pl.semaphore_wait(descend, 1)
+
+    @pl.when(below)
+    def _():
+        pl.semaphore_signal(descend, inc=1, device_id={"tp": z - 1}, device_id_type=MESH)
+
     w_in.wait()
     a_all.wait_recv()
     attended[...] = att[...].astype(jnp.float32)
@@ -312,6 +332,7 @@
             pltpu.VMEM((NDEV, 4, BLK), jnp.float32),
             pltpu.VMEM((NTP, 2, 256), jnp.float32),
             pltpu.VMEM((NTP, 2, 256), jnp.float32),
+            pltpu.SemaphoreType.REGULAR, pltpu.SemaphoreType.REGULAR,
             dma((9,)), dma((2,)), dma((2,)), dma((2,)), dma((2,)), dma((2,)), dma((2,)),
         ],
         compiler_params=pltpu.CompilerParams(

time: 63.2 us -> 58.7 us (0.929)
  Pallas kernels: 62.5 us -> 57.9 us
    pallas_call x1, Pallas kernels: 59.9 us -> 55.4 us  [per_device(): pl.pallas_call(exchange_kernel, out_shape=(jax.ShapeDtypeStruct((NDEV, 51...]
where the time goes in v5:
time: 58.7 us; the launch traced here: 58.6 us
  Pallas kernels  57.9 us (99%)
  between operations  0.64 us (1%)
    pallas_call x1, Pallas kernels, per_device(): pl.pallas_call(exchange_kernel, out_shape=(jax.ShapeDtypeStruct((NDEV, 51...  55.4 us
    pallas_call x1, Pallas kernels, per_device(): pl.pallas_call(place_kernel, out_shape=(jax.ShapeDtypeStruct((64, 256, BL...  2.53 us

profile of v5, /device:TPU:1, one launch (start us, length us, event | category | flops | bytes accessed | tf_op | source)
XLA Modules:
  0.0 58.6 jit_solution(610130904672170555)
XLA Ops:
  0.6 55.4 %shard_map.85 = (bf16[32,512,128]{2,1,0:T(8,128)(2,1)S(1)}, bf16[2,256]{1,0:T(2,128)(2,1)S(1)}, bf16[2,2,32]{2,1,0:T(2,128)(2,1)S(1)}, s32[1,128]{1,0:T(1,128)S(1)}) custom-call(s32[16,128]{1,0:T(8,128)} %table_hbm.1, s32[16]{0:T(128)} %lengths_hbm.1, bf16[2,64]{1,0:T(2,128)(2,1)} %bitcast.15, bf16[64,256,128]{2,1,0:T(8,128)(2,1)} %bitcast.13, ...), custom_call_target="tpu_custom_call" | custom-call | tf_op jit(solution)/shard_map/pallas_call | solution.py:302
  56.0 2.5 %shard_map.86 = (bf16[64,256,128]{2,1,0:T(8,128)(2,1)}, bf16[2,256]{1,0:T(2,128)(2,1)}, bf16[2,2,32]{2,1,0:T(2,128)(2,1)}) custom-call(s32[1,128]{1,0:T(1,128)S(1)} %get-tuple-element.10.src, bf16[64,256,128]{2,1,0:T(8,128)(2,1)S(1)} %bitcast.12, bf16[2,256]{1,0:T(2,128)(2,1)S(1)} %get-tuple-element.12.summed, bf16[2,2,32]{2,1,0:T(2,128)(2,1)S(1)} %get-tuple-element.13.scales), custom_call_target="tpu_custom_call" | custom-call | tf_op jit(solution)/shard_map/pallas_call | solution.py:348

commit v6 on v5

--- a/solution.py
+++ b/solution.py
@@ -14,9 +14,7 @@
 NDEV = NSEQ * NGRP
 BLK = 128
 ROOT = 1.0 / math.sqrt(128.0)
-START = (0, 256, 128, 384)
-
-
+HALF = 64
 PEERS = [
     (dy, (dy + turn) % 4, dc)
     for turn in range(4) for dy in range(4) for dc in range(2)
@@ -26,10 +24,10 @@
 
 def exchange_kernel(
     table_hbm, lengths_hbm, scale_hbm, pool_hbm, q_hbm, w_hbm,
-    arr, out_ref, scale_out, place_out,
+    out, out_ref, scale_out,
     table, scale_in, codes_v, scales_v, codes, scal, lens,
-    pool_k, pool_v, send, q_ref, qall, w, pmsg, part, smsg, stat, amsg, att, attended, pout, zbuf,
-    climb, descend, in_sem, q_sem, b_sem, p_sem, s_sem, a_sem, z_sem,
+    place_v, place, pool_k, pool_v, send_k, send_v0, send_v1, arr_k, arr_v0, arr_v1, q_ref, qall, w, pmsg, part, smsg, stat, amsg, att, attended, pout, zbuf,
+    climb, descend, in_sem, q_sem, k_sem, v0_sem, v1_sem, p_sem, s_sem, a_sem, z_sem,
 ):
     y = lax.axis_index("seq")
     z = lax.axis_index("tp")
@@ -53,7 +51,8 @@
     w_in = pltpu.make_async_copy(w_hbm, w, in_sem.at[6])
     codes_out = pltpu.make_async_copy(codes_v, codes, in_sem.at[7])
     scales_out = pltpu.make_async_copy(scales_v, scal, in_sem.at[8])
-    for copy in (table_in, q_in, keys_in, scales_in, lens_in, vals_in, w_in):
+    place_in = pltpu.make_async_copy(place_v, place, in_sem.at[9])
+    for copy in (table_in, keys_in, q_in, scales_in, lens_in):
         copy.start()
 
     barrier = pltpu.get_barrier_semaphore()
@@ -97,20 +96,18 @@
     def code_of(q, gg, r):
         return codes[2 * gg, q + 4 * r]
 
-    def pick_one(c, ty, tg):
-        pool, r = (pool_k, pool_v)[c // 2], c % 2
-        slot = (code_of(ty, tg, r) >> 6) & 63
-        send[ty * NGRP + tg, pl.ds(START[c], BLK), :] = pool[slot]
-
-    def pick(c):
-        pool, r = (pool_k, pool_v)[c // 2], c % 2
-
-        def body(t, carry):
-            slot = (code_of(t // NGRP, t % NGRP, r) >> 6) & 63
-            send[t, pl.ds(START[c], BLK), :] = pool[slot]
-            return carry
-
-        lax.fori_loop(0, NDEV, body, 0)
+    def slot_of(ty, tg, r):
+        return (code_of(ty, tg, r) >> 6) & 63
+
+    def pick_keys(r, ty, tg):
+        send_k[2 * (ty * NGRP + tg) + r] = pool_k[slot_of(ty, tg, r)]
+
+    def pick_values(t, carry):
+        for r in range(2):
+            slot = slot_of(t // NGRP, t % NGRP, r)
+            send_v0[2 * t + r] = pool_v[slot, pl.ds(0, HALF), :]
+            send_v1[2 * t + r] = pool_v[slot, pl.ds(HALF, HALF), :]
+        return carry
 
     def remote(src, dst, sems, device):
         return pltpu.make_async_remote_copy(
@@ -118,33 +115,46 @@
             device_id=device, device_id_type=MESH,
         )
 
-    def send_wave(c):
-        rows = pl.ds(START[c], BLK)
+    def send_keys(r, ty, tg):
+        device = {"seq": ty, "grp": tg}
+        remote(send_k.at[2 * (ty * NGRP + tg) + r], arr_k.at[2 * me + r], k_sem, device).start()
+
+    def send_values(src, dst, sems):
         for offset in PEERS:
             ty, tg = peer(offset)
-            remote(send.at[ty * NGRP + tg, rows], arr.at[me, rows], b_sem, {"seq": ty, "grp": tg}).start()
+            theirs, mine = pl.ds(2 * (ty * NGRP + tg), 2), pl.ds(2 * me, 2)
+            remote(src.at[theirs], dst.at[mine], sems, {"seq": ty, "grp": tg}).start()
 
     here = {"seq": ys[1]}
     rest = pl.ds(0, NDEV - 1)
     q_all = remote(qall.at[pl.ds(0, NGRP - 1)], qall.at[pl.ds(0, NGRP - 1)], q_sem, here)
-    b_all = remote(send.at[rest], arr.at[rest], b_sem, here)
+    both = pl.ds(0, 2 * (NDEV - 1))
+    k_all = remote(send_k.at[both], arr_k.at[both], k_sem, here)
+    v0_all = remote(send_v0.at[both], arr_v0.at[both], v0_sem, here)
+    v1_all = remote(send_v1.at[both], arr_v1.at[both], v1_sem, here)
     p_all = remote(pmsg.at[rest], part.at[rest], p_sem, here)
     s_all = remote(stat.at[rest], stat.at[rest], s_sem, here)
     a_all = remote(att.at[rest], att.at[rest], a_sem, here)
     z_all = remote(pout.at[pl.ds(0, NTP - 1)], zbuf.at[pl.ds(0, NTP - 1)], z_sem, here)
 
     keys_in.wait()
-    for offset in PEERS:
-        pick_one(0, *peer(offset))
+    vals_in.start()
+    w_in.start()
+    ahead = 6
+    for offset in PEERS[:ahead]:
+        pick_keys(0, *peer(offset))
     pl.semaphore_wait(barrier, NDEV - 1 + jnp.where(above, 1, 0) + jnp.where(below, 1, 0))
     for k in range(1, NGRP):
         remote(q_ref, qall.at[g], q_sem, {"grp": (g + k) % NGRP}).start()
-    send_wave(0)
-    pick_one(0, y, g)
-    pick(1)
+    for i, offset in enumerate(PEERS):
+        if i + ahead < len(PEERS):
+            pick_keys(0, *peer(PEERS[i + ahead]))
+        send_keys(0, *peer(offset))
+    pick_keys(0, y, g)
+    for offset in PEERS + [(0, 0, 0)]:
+        pick_keys(1, *peer(offset))
     vals_in.wait()
-    pick(2)
-    pick(3)
+    lax.fori_loop(0, NDEV, pick_values, 0)
     scales_out.wait()
     lens_in.wait()
     q_all.wait_recv()
@@ -158,7 +168,7 @@
             t, r = (n // 2) * NGRP + gg, n % 2
             found_at = code_of(n // 2, gg, r)
             slot, row, column = (found_at >> 6) & 63, (found_at >> 5) & 1, (n // 2) * 32 + (found_at & 31)
-            keys = send[t, pl.ds(r * 256, BLK), :]
+            keys = send_k[2 * t + r]
             s = lax.dot_general(q, keys, (((1,), (1,)), ((), ())), preferred_element_type=jnp.float32)
             s = s * (scal[0, slot] * ROOT)
             value_scales.append(scal[1, slot])
@@ -176,7 +186,8 @@
             weight = jnp.where(masks[n], jnp.exp(scores[n] - peak), 0.0)
             total = total + weight
             scaled = (weight * value_scales[n]).astype(jnp.bfloat16)
-            acc = acc + jnp.dot(scaled, send[t, pl.ds(r * 256 + BLK, BLK), :], preferred_element_type=jnp.float32)
+            values = jnp.concatenate([send_v0[2 * t + r], send_v1[2 * t + r]], axis=0)
+            acc = acc + jnp.dot(scaled, values, preferred_element_type=jnp.float32)
         denom = jnp.sum(total, axis=1, keepdims=True)
         line = jnp.where(lane16 == row16, peak, jnp.where(lane16 == row16 + 16, denom, 0.0))
         line = jnp.sum(line, axis=0, keepdims=True)
@@ -196,7 +207,8 @@
         remote(pmsg.at[ty * NGRP + tg], part.at[me], p_sem, {"seq": ty, "grp": tg}).start()
     part[me] = pmsg[me]
     stat[me] = smsg[g]
-    send_wave(1)
+    for offset in PEERS:
+        send_keys(1, *peer(offset))
     s_all.wait_recv()
     p_all.wait_recv()
 
@@ -216,9 +228,10 @@
     for offset in PEERS:
         ty, tg = peer(offset)
         remote(amsg, att.at[(y % 2) * 16 + g * 2 + y // 2], a_sem, {"seq": ty, "grp": tg}).start()
-    send_wave(2)
-    send_wave(3)
-    arr[me] = send[me]
+    send_values(send_v0, arr_v0, v0_sem)
+    send_values(send_v1, arr_v1, v1_sem)
+    for sent, arrived in ((send_k, arr_k), (send_v0, arr_v0), (send_v1, arr_v1)):
+        arrived[pl.ds(2 * me, 2)] = sent[pl.ds(2 * me, 2)]
     wide = lax.broadcasted_iota(jnp.int32, (8, BLK), 1)
     first = pltpu.roll(jnp.broadcast_to(table[pl.ds(2 * g, 1), :], (8, BLK)), (BLK - 32 * y) % BLK, 1)
     second = pltpu.roll(jnp.broadcast_to(table[pl.ds(2 * g + 1, 1), :], (8, BLK)), (BLK + 32 - 32 * y) % BLK, 1)
@@ -228,7 +241,8 @@
     inside = lax.broadcasted_iota(jnp.int32, (BLK, BLK), 0) < 64
     before = inside & ((down >> 6) == (across >> 6)) & (down < across)
     rank = jnp.sum(before.astype(jnp.int32), axis=0, keepdims=True)
-    place_out[...] = ((own >> 6) * 2 + rank) & 63
+    place_v[...] = ((own >> 6) * 2 + rank) & 63
+    place_in.start()
     owner = lax.broadcasted_iota(jnp.int32, (NDEV, BLK), 0)
     hot = (owner == (own >> 6)).astype(jnp.float32).astype(jnp.bfloat16)
     flat = stat[...].reshape(NDEV, BLK).T.astype(jnp.bfloat16)
@@ -270,45 +284,50 @@
     z_all.wait_recv()
     out_ref[...] = jnp.sum(zbuf[...], axis=0).astype(jnp.bfloat16)
 
-    for phase in (q_all, s_all, p_all, a_all, z_all, b_all):
+    place_in.wait()
+
+    def settle(arrived, start, length):
+        def body(p, carry):
+            out[p, pl.ds(start, length), :] = arrived[place[0, p]]
+            return carry
+
+        lax.fori_loop(0, 64, body, 0, unroll=8)
+
+    k_all.wait_recv()
+    settle(arr_k, 0, BLK)
+    v0_all.wait_recv()
+    settle(arr_v0, BLK, HALF)
+    for phase in (q_all, s_all, p_all, a_all, z_all, k_all, v0_all, v1_all):
         phase.wait_send()
-    b_all.wait_recv()
-
-
-def place_kernel(src, arr, summed, scales, out, out_sum, out_scales, sem):
-    small = (
+    v1_all.wait_recv()
+    settle(arr_v1, BLK + HALF, HALF)
+
+
+def write_kernel(cache, summed, scales, out, out_sum, out_scales, sem):
+    copies = [
+        pltpu.make_async_copy(cache, out, sem.at[0]),
         pltpu.make_async_copy(summed, out_sum, sem.at[1]),
         pltpu.make_async_copy(scales, out_scales, sem.at[2]),
-    )
-    for copy in small:
+    ]
+    for copy in copies:
         copy.start()
-
-    def put(p, carry):
-        pltpu.make_async_copy(arr.at[src[0, p]], out.at[p], sem.at[0]).start()
-        return carry
-
-    lax.fori_loop(0, 64, put, 0, unroll=8)
-    for copy in small:
+    for copy in copies:
         copy.wait()
-    pltpu.make_async_copy(arr, out, sem.at[0]).wait()
 
 
 def per_device(queries, cache_pool, block_scale, block_table, lengths, output_weight):
     vmem = pl.BlockSpec(memory_space=pltpu.VMEM)
-    smem = pl.BlockSpec(memory_space=pltpu.SMEM)
     hbm = pl.BlockSpec(memory_space=pltpu.HBM)
-    anywhere = pl.BlockSpec(memory_space=pl.ANY)
     dma = pltpu.SemaphoreType.DMA
-    arrived, summed, scales, place = pl.pallas_call(
+    cache, summed, scales = pl.pallas_call(
         exchange_kernel,
         out_shape=(
-            jax.ShapeDtypeStruct((NDEV, 512, BLK), jnp.bfloat16),
+            jax.ShapeDtypeStruct((64, 256, BLK), jnp.bfloat16),
             jax.ShapeDtypeStruct((2, 256), jnp.bfloat16),
             jax.ShapeDtypeStruct((2, 2, 32), jnp.bfloat16),
-            jax.ShapeDtypeStruct((1, BLK), jnp.int32),
         ),
         in_specs=[hbm] * 6,
-        out_specs=(vmem, vmem, vmem, vmem),
+        out_specs=(vmem, vmem, vmem),
         scratch_shapes=[
             pltpu.VMEM((16, BLK), jnp.int32),
             pltpu.VMEM((2, 64), jnp.bfloat16),
@@ -317,9 +336,16 @@
             pltpu.SMEM((16, BLK), jnp.int32),
             pltpu.SMEM((2, 64), jnp.float32),
             pltpu.SMEM((16,), jnp.int32),
+            pltpu.VMEM((1, BLK), jnp.int32),
+            pltpu.SMEM((1, BLK), jnp.int32),
             pltpu.VMEM((64, BLK, BLK), jnp.bfloat16),
             pltpu.VMEM((64, BLK, BLK), jnp.bfloat16),
-            pltpu.VMEM((NDEV, 512, BLK), jnp.bfloat16),
+            pltpu.VMEM((64, BLK, BLK), jnp.bfloat16),
+            pltpu.VMEM((64, HALF, BLK), jnp.bfloat16),
+            pltpu.VMEM((64, HALF, BLK), jnp.bfloat16),
+            pltpu.VMEM((64, BLK, BLK), jnp.bfloat16),
+            pltpu.VMEM((64, HALF, BLK), jnp.bfloat16),
+            pltpu.VMEM((64, HALF, BLK), jnp.bfloat16),
             pltpu.VMEM((16, BLK), jnp.bfloat16),
             pltpu.VMEM((NGRP, 16, BLK), jnp.bfloat16),
             pltpu.VMEM((1024, 256), jnp.bfloat16),
@@ -333,7 +359,7 @@
             pltpu.VMEM((NTP, 2, 256), jnp.float32),
             pltpu.VMEM((NTP, 2, 256), jnp.float32),
             pltpu.SemaphoreType.REGULAR, pltpu.SemaphoreType.REGULAR,
-            dma((9,)), dma((2,)), dma((2,)), dma((2,)), dma((2,)), dma((2,)), dma((2,)),
+            dma((10,)), dma((2,)), dma((2,)), dma((2,)), dma((2,)), dma((2,)), dma((2,)), dma((2,)), dma((2,)),
         ],
         compiler_params=pltpu.CompilerParams(
             collective_id=0, has_side_effects=True, vmem_limit_bytes=24 << 20
@@ -346,17 +372,17 @@
         )
     ))
     decode_cache, attention_output, decode_scale = pl.pallas_call(
-        place_kernel,
+        write_kernel,
         out_shape=(
             jax.ShapeDtypeStruct((64, 256, BLK), jnp.bfloat16),
             jax.ShapeDtypeStruct((2, 256), jnp.bfloat16),
             jax.ShapeDtypeStruct((2, 2, 32), jnp.bfloat16),
         ),
-        in_specs=[smem, vmem, vmem, vmem],
+        in_specs=[vmem, vmem, vmem],
         out_specs=(hbm, hbm, hbm),
         scratch_shapes=[dma((3,))],
         compiler_params=pltpu.CompilerParams(vmem_limit_bytes=12 << 20),
-    )(place, arrived.reshape(64, 256, BLK), summed, scales)
+    )(cache, summed, scales)
     return (
         attention_output,
         decode_cache.reshape(2, 32, 1, 2, BLK, BLK),

time: 58.7 us -> 58.4 us (level)
  no operation moved by 1% of the time
where the time goes in v6:
time: 58.4 us; the launch traced here: 58.2 us
  Pallas kernels  57.6 us (99%)
  between operations  0.64 us (1%)
    pallas_call x1, Pallas kernels, per_device(): pl.pallas_call(exchange_kernel, out_shape=(jax.ShapeDtypeStruct((64, 256,...  55.5 us
    pallas_call x1, Pallas kernels, per_device(): pl.pallas_call(write_kernel, out_shape=(jax.ShapeDtypeStruct((64, 256, BL...  2.05 us

profile of v6, /device:TPU:1, one launch (start us, length us, event | category | flops | bytes accessed | tf_op | source)
XLA Modules:
  0.0 58.2 jit_solution(7323633721712518912)
XLA Ops:
  0.6 55.5 %shard_map.85 = (bf16[64,256,128]{2,1,0:T(8,128)(2,1)S(1)}, bf16[2,256]{1,0:T(2,128)(2,1)S(1)}, bf16[2,2,32]{2,1,0:T(2,128)(2,1)S(1)}) custom-call(s32[16,128]{1,0:T(8,128)} %table_hbm.1, s32[16]{0:T(128)} %lengths_hbm.1, bf16[2,64]{1,0:T(2,128)(2,1)} %bitcast.13, bf16[64,256,128]{2,1,0:T(8,128)(2,1)} %bitcast.11, bf16[16,128]{1,0:T(8,128)(2,1)} %bitcast.12, ...), custom_call_target="tpu_custom_call" | custom-call | tf_op jit(solution)/shard_map/pallas_call | solution.py:322
  56.2 2.0 %shard_map.86 = (bf16[64,256,128]{2,1,0:T(8,128)(2,1)}, bf16[2,256]{1,0:T(2,128)(2,1)}, bf16[2,2,32]{2,1,0:T(2,128)(2,1)}) custom-call(bf16[64,256,128]{2,1,0:T(8,128)(2,1)S(1)} %get-tuple-element.9.cache, bf16[2,256]{1,0:T(2,128)(2,1)S(1)} %get-tuple-element.10.summed, bf16[2,2,32]{2,1,0:T(2,128)(2,1)S(1)} %get-tuple-element.11.scales), custom_call_target="tpu_custom_call" | custom-call | tf_op jit(solution)/shard_map/pallas_call | solution.py:374

commit v7 on v6

--- a/solution.py
+++ b/solution.py
@@ -20,6 +20,9 @@
     for turn in range(4) for dy in range(4) for dc in range(2)
     if (dy, turn, dc) != (0, 0, 0)
 ]
+
+PEERS = [o for a in PEERS for o in (a, (-a[0] % 4, -a[1] % 4, a[2]))]
+PEERS = list(dict.fromkeys(PEERS))
 
 
 def exchange_kernel(
@@ -153,6 +156,8 @@
     pick_keys(0, y, g)
     for offset in PEERS + [(0, 0, 0)]:
         pick_keys(1, *peer(offset))
+    for offset in PEERS[:12]:
+        send_keys(1, *peer(offset))
     vals_in.wait()
     lax.fori_loop(0, NDEV, pick_values, 0)
     scales_out.wait()
@@ -207,7 +212,7 @@
         remote(pmsg.at[ty * NGRP + tg], part.at[me], p_sem, {"seq": ty, "grp": tg}).start()
     part[me] = pmsg[me]
     stat[me] = smsg[g]
-    for offset in PEERS:
+    for offset in PEERS[12:]:
         send_keys(1, *peer(offset))
     s_all.wait_recv()
     p_all.wait_recv()
@@ -291,7 +296,7 @@
             out[p, pl.ds(start, length), :] = arrived[place[0, p]]
             return carry
 
-        lax.fori_loop(0, 64, body, 0, unroll=8)
+        lax.fori_loop(0, 64, body, 0, unroll=True)
 
     k_all.wait_recv()
     settle(arr_k, 0, BLK)

time: 58.4 us -> 58.8 us (level)
  no operation moved by 1% of the time
where the time goes in v7:
time: 58.8 us; the launch traced here: 58.7 us
  Pallas kernels  58 us (99%)
  between operations  0.64 us (1%)
    pallas_call x1, Pallas kernels, per_device(): pl.pallas_call(exchange_kernel, out_shape=(jax.ShapeDtypeStruct((64, 256,...  56 us
    pallas_call x1, Pallas kernels, per_device(): pl.pallas_call(write_kernel, out_shape=(jax.ShapeDtypeStruct((64, 256, BL...  2.05 us

profile of v7, /device:TPU:1, one launch (start us, length us, event | category | flops | bytes accessed | tf_op | source)
XLA Modules:
  0.0 58.7 jit_solution(2715653648641529461)
XLA Ops:
  0.6 56.0 %shard_map.85 = (bf16[64,256,128]{2,1,0:T(8,128)(2,1)S(1)}, bf16[2,256]{1,0:T(2,128)(2,1)S(1)}, bf16[2,2,32]{2,1,0:T(2,128)(2,1)S(1)}) custom-call(s32[16,128]{1,0:T(8,128)} %table_hbm.1, s32[16]{0:T(128)} %lengths_hbm.1, bf16[2,64]{1,0:T(2,128)(2,1)} %bitcast.13, bf16[64,256,128]{2,1,0:T(8,128)(2,1)} %bitcast.11, bf16[16,128]{1,0:T(8,128)(2,1)} %bitcast.12, ...), custom_call_target="tpu_custom_call" | custom-call | tf_op jit(solution)/shard_map/pallas_call | solution.py:327
  56.6 2.0 %shard_map.86 = (bf16[64,256,128]{2,1,0:T(8,128)(2,1)}, bf16[2,256]{1,0:T(2,128)(2,1)}, bf16[2,2,32]{2,1,0:T(2,128)(2,1)}) custom-call(bf16[64,256,128]{2,1,0:T(8,128)(2,1)S(1)} %get-tuple-element.9.cache, bf16[2,256]{1,0:T(2,128)(2,1)S(1)} %get-tuple-element.10.summed, bf16[2,2,32]{2,1,0:T(2,128)(2,1)S(1)} %get-tuple-element.11.scales), custom_call_target="tpu_custom_call" | custom-call | tf_op jit(solution)/shard_map/pallas_call | solution.py:379
